TPU v7x, 32 devices: a whole 2x2x4 slice. The times are simulated.
32 devices in a mesh: atm: 4 (over z), land: 8 (over y, x, core).
Axes of the slice: x: 2, y: 2, z: 4, core: 2. Of those that a mesh axis runs over, the one named last changes fastest.
Arguments:
- tile_forcing: bfloat16 [4096, 128], P(('atm', 'land')), may hold values from -6 to 6
- elevation_gap: float32 [65536], P(('atm', 'land')), may hold values from -5 to 5
- lapse_rate: float32 [128], replicated, may hold values from -3 to 3
- column_tile: int32 [65536], P(('atm', 'land')), may hold values from 0 to 127
- column_target: int32 [65536], P(('atm', 'land')), may hold values from 0 to 163839, as said below
- owner_counts: int32 [32], P(('atm', 'land')), may hold values from 1 to 5120, as said below
- land_state: float32 [163840, 128], P(('atm', 'land')), may hold values from -6 to 6
- w_in: bfloat16 [256, 1024], replicated, may hold values from -0.375 to 0.375
- norm_gains: float32 [2, 1024], replicated, may hold values from 0.5 to 1.5
- w_up: bfloat16 [1, 1024, 1024], replicated, may hold values from -0.1875 to 0.1875
- w_down: bfloat16 [1, 1024, 1024], replicated, may hold values from -0.1875 to 0.1875
- w_out: bfloat16 [1024, 256], replicated, may hold values from -0.1875 to 0.1875
Outputs:
- new_state: float32 [163840, 128], P(('atm', 'land'))
- tile_flux: float32 [4096, 128], P(('atm', 'land'))
Inputs may be any that keep to these rules, and one draw needn't show every extreme that they name: `column_target`: live slots of owner j are j * 5120 to j * 5120 + owner_counts[j] - 1; every live slot is named by exactly one column and no other slot is named. The columns of one device name at most 161 slots of any one owner, and some pair reaches 161. `owner_counts`: they sum to 65536; the largest is exactly 5120. `column_tile`: index of the column's tile among the 128 tiles of the device that holds the column.
All inputs are finite; a program needn't handle non-finite values.
Results may differ from a plain program's by a relative error of at most 0.0038.
Values may be sent and summed in bfloat16 or wider, within the bound.
No kernel may reach another device: no remote copies, remote signals or barrier semaphores. Data moves between devices by JAX's collectives and lax.ppermute only.
A program may use at most 128 MiB of HBM per device.

v0:
```python
import functools

import jax
import jax.numpy as jnp
from jax import lax
from jax.experimental import pallas as pl
from jax.experimental.pallas import tpu as pltpu
from jax.sharding import PartitionSpec as P


AXES = ("atm", "land")
ROWS = 256
FIELDS = 8
VMEM = pl.BlockSpec(memory_space=pltpu.VMEM)
SMEM = pl.BlockSpec(memory_space=pltpu.SMEM)
BF16 = jnp.bfloat16
F32 = jnp.float32


def iota(shape, dim):
    return lax.broadcasted_iota(jnp.int32, shape, dim)


def dot_nt(a, b):
    return lax.dot_general(a, b, (((1,), (1,)), ((), ())), preferred_element_type=F32)


def cost(microseconds):
    return pl.CostEstimate(
        flops=int(microseconds * 8e6), bytes_accessed=int(microseconds * 2e6), transcendentals=0
    )


def bucket_kernel(devices, capacity, tgt_ref, tile_ref, gap_ref, out_ref, count_ref):
    columns = tgt_ref.shape[1]
    places = out_ref.shape[1]
    tiles = count_ref.shape[0]
    target = tgt_ref[...]
    peer = jnp.floor((target.astype(F32) + 0.5) * (1.0 / capacity)).astype(jnp.int32)
    slot = target - peer * capacity
    high, low = lax.shift_right_logical(slot, 8), slot & (ROWS - 1)
    tile = tile_ref[...]
    gap = gap_ref[...]
    gap1 = gap.astype(BF16).astype(F32)
    gap2 = (gap - gap1).astype(BF16).astype(F32)
    gap3 = gap - gap1 - gap2
    hot = iota((devices, columns), 0) == peer
    hot_f = jnp.where(hot, 1.0, 0.0)
    hot_b = hot_f.astype(BF16)
    block = min(256, columns)
    upper = jnp.where(iota((block, block), 0) <= iota((block, block), 1), 1.0, 0.0).astype(BF16)
    carry = jnp.zeros((devices, 1), F32)
    ranks = []
    for start in range(0, columns, block):
        part = hot_b[:, start : start + block]
        inside = jnp.dot(part, upper, preferred_element_type=F32)
        here = inside + carry
        ranks.append(jnp.sum(here * hot_f[:, start : start + block], axis=0, keepdims=True))
        carry = carry + inside[:, block - 1 : block]
    rank = jnp.concatenate(ranks, axis=1).astype(jnp.int32) - 1
    place_hot = jnp.where(iota((places, columns), 0) == rank, 1.0, 0.0).astype(BF16)
    zero = jnp.zeros((1, columns), F32)
    fields = jnp.concatenate(
        [
            high.astype(F32) + 1.0,
            low.astype(F32),
            tile.astype(F32),
            gap1,
            gap2,
            gap3,
            zero,
            zero,
        ],
        axis=0,
    )
    spread = jnp.concatenate(
        [jnp.where(peer == device, fields, 0.0) for device in range(devices)], axis=0
    ).astype(BF16)
    out_ref[...] = dot_nt(spread, place_hot).astype(BF16)
    tile_hot = jnp.where(iota((tiles, columns), 0) == tile, 1.0, 0.0).astype(BF16)
    count_ref[...] = jnp.dot(
        tile_hot, jnp.ones((columns, count_ref.shape[1]), BF16), preferred_element_type=F32
    )


def arrange_kernel(devices, tiles, me_ref, got_ref, mine_ref, guest_ref):
    places = got_ref.shape[1]
    rows = mine_ref.shape[1]
    total = jnp.zeros((5 * rows, ROWS), F32)
    row_id = iota((rows, places), 0).astype(F32) + 1.0
    low_id = iota((ROWS, places), 0).astype(F32)
    for device in range(devices):
        got = got_ref[device * FIELDS : (device + 1) * FIELDS, :].astype(F32)
        hot = got[0:1] == row_id
        zero = jnp.zeros((rows, places), F32)
        parts = [jnp.where(hot, float(device + 1), zero)]
        parts += [jnp.where(hot, got[field : field + 1], zero) for field in (2, 3, 4, 5)]
        left = jnp.concatenate(parts, axis=0).astype(BF16)
        right = jnp.where(low_id == got[1:2], 1.0, 0.0).astype(BF16)
        total = total + dot_nt(left, right)
    source = total[0:rows].astype(jnp.int32) - 1
    tile = total[rows : 2 * rows].astype(jnp.int32)
    gap = total[2 * rows : 3 * rows] + total[3 * rows : 4 * rows] + total[4 * rows :]
    for out_ref, me in ((mine_ref, me_ref[0]), (guest_ref, me_ref[0] ^ 1)):
        row = table_row(devices, tiles, source ^ me, tile)
        out_ref[0] = jnp.where(source >= 0, row, devices * tiles).astype(F32)
        out_ref[1] = gap


def table_row(devices, tiles, relative, tile):
    groups, half = devices // 2, tiles // 2
    far = groups // 4
    group = (lax.shift_right_logical(relative, 1) & 3) * far + lax.shift_right_logical(relative, 3)
    part = jnp.where(tile >= half, 1, 0)
    return (relative & 1) * (groups * tiles) + part * (groups * half) + group * half + (tile - part * half)


def tile_ranges(own, other):
    have = (own + (ROWS - 1)) // ROWS
    return jnp.maximum(own - other, 0) // (2 * ROWS), have


def network_kernel(
    own_ref,
    other_ref,
    state_ref,
    guest_ref,
    mine_ref,
    guest_mine_ref,
    even_ref,
    odd_ref,
    lapse_ref,
    w_in_ref,
    gains_ref,
    w_up_ref,
    w_down_ref,
    w_out_ref,
    tend_ref,
    guest_tend_ref,
    keep_ref,
    send_ref,
    table_ref,
    first_ref,
    second_ref,
    rows_ref,
    flux_ref,
    x_ref,
    gap_ref,
    index_ref,
    scalar_ref,
    sem,
):
    half = even_ref.shape[0]
    width = even_ref.shape[1]
    spare = 2 * half
    given, have = tile_ranges(own_ref[0], other_ref[0])
    taken, _ = tile_ranges(other_ref[0], own_ref[0])
    own_tiles = have - given
    all_tiles = own_tiles + taken
    lines = mine_ref.shape[1]
    last_line = 2 * lines

    index_ref[0:lines, :] = mine_ref[0].astype(jnp.int32)
    index_ref[lines:last_line, :] = guest_mine_ref[0].astype(jnp.int32)
    index_ref[last_line:, :] = jnp.full_like(index_ref[last_line:, :], spare)
    copy = pltpu.make_async_copy(index_ref, scalar_ref, sem)
    copy.start()
    table_ref[0:half, :] = even_ref[...].astype(F32)
    table_ref[half:spare, :] = odd_ref[...].astype(F32)
    table_ref[spare:, :] = jnp.zeros_like(table_ref[spare:, :])
    first_ref[...] = jnp.zeros_like(first_ref)
    second_ref[...] = jnp.zeros_like(second_ref)
    copy.wait()

    def norm(values, gain):
        scale = lax.rsqrt(jnp.mean(values * values, axis=-1, keepdims=True) + 1e-06)
        return (values * scale * gain).astype(BF16)

    def place_of(step):
        is_own = step < own_tiles
        index = jnp.where(is_own, step + given, step - own_tiles)
        index = jnp.where(step < all_tiles, index, 0)
        return is_own, index, pl.multiple_of(index * ROWS, ROWS)

    def line_of(step):
        is_own, index, _ = place_of(step)
        line = jnp.where(is_own, index, index + lines)
        return jnp.where((step >= 0) & (step < all_tiles), line, last_line)

    def fetch(step):
        for chain in range(2):
            line = line_of(2 * step + chain)
            for row in range(ROWS):
                at = chain * ROWS + row
                rows_ref[at : at + 1, :] = table_ref[pl.ds(scalar_ref[line, row], 1), :]

    def spread(step):
        for chain in range(2):
            line = line_of(2 * step + chain)
            for row in range(ROWS):
                at = chain * ROWS + row
                bank = second_ref if row % 2 else first_ref
                where = pl.ds(scalar_ref[line, row], 1)
                bank[where, :] = bank[where, :] + flux_ref[at : at + 1, :]

    def load(chain, step):
        is_own, index, start = place_of(step)

        @pl.when(is_own)
        def _():
            x_ref[chain] = state_ref[pl.ds(start, ROWS), :].astype(BF16)
            gap_ref[chain] = jnp.broadcast_to(mine_ref[1, pl.ds(index, 1), :], (8, ROWS))

        @pl.when(jnp.logical_not(is_own))
        def _():
            x_ref[chain] = guest_ref[pl.ds(start, ROWS), :]
            gap_ref[chain] = jnp.broadcast_to(guest_mine_ref[1, pl.ds(index, 1), :], (8, ROWS))

    def store(step, tend):
        is_own, _, start = place_of(step)

        @pl.when(is_own)
        def _():
            tend_ref[pl.ds(start, ROWS), :] = tend

        @pl.when(jnp.logical_not(is_own) & (step < all_tiles))
        def _():
            guest_tend_ref[pl.ds(start, ROWS), :] = tend

    def two_tiles(step, _):
        chains = range(2)
        for chain in chains:
            load(chain, 2 * step + chain)
        inputs = []
        for chain in chains:
            gap = jnp.transpose(gap_ref[chain])[:, 0:1]
            forcing = rows_ref[chain * ROWS : (chain + 1) * ROWS, :] + gap * lapse_ref[...]
            inputs.append(jnp.concatenate([forcing.astype(BF16), x_ref[chain]], axis=1))
        fetch(step + 1)
        spread(step - 1)
        h = [jnp.dot(v, w_in_ref[...], preferred_element_type=F32) for v in inputs]
        low = [norm(v, gains_ref[0:1, :]) for v in h]
        up = [jnp.dot(v, w_up_ref[...], preferred_element_type=F32) for v in low]
        active = [(v * (0.5 + 0.5 * jnp.tanh(0.5 * v))).astype(BF16) for v in up]
        h = [
            v + jnp.dot(a, w_down_ref[...], preferred_element_type=F32) for v, a in zip(h, active)
        ]
        low = [norm(v, gains_ref[1:2, :]) for v in h]
        result = [jnp.dot(v, w_out_ref[...], preferred_element_type=F32) for v in low]
        for chain in chains:
            flux_ref[chain * ROWS : (chain + 1) * ROWS, :] = (
                result[chain][:, width:].astype(BF16).astype(F32)
            )
        for chain in chains:
            store(2 * step + chain, result[chain][:, :width].astype(BF16))
        return 0

    steps = (all_tiles + 1) // 2
    fetch(0)
    lax.fori_loop(0, steps, two_tiles, 0)
    spread(steps - 1)
    keep_ref[...] = first_ref[0:half, :] + second_ref[0:half, :]
    send_ref[...] = (first_ref[half:spare, :] + second_ref[half:spare, :]).astype(BF16)


def add_near(keep_ref, in_ref, first_ref, first_out_ref, second_ref, second_out_ref):
    for other in range(2):
        first_ref[other] = keep_ref[0, other, 0] + in_ref[0, other, 0].astype(F32)
        second_ref[other] = keep_ref[1, 0, other] + in_ref[1, 0, other].astype(F32)
        first_out_ref[other] = (keep_ref[0, other, 1] + in_ref[0, other, 1].astype(F32)).astype(BF16)
        second_out_ref[other] = (keep_ref[1, 1, other] + in_ref[1, 1, other].astype(F32)).astype(BF16)


def add_next(a_ref, a_in_ref, b_ref, b_in_ref, first_ref, first_out_ref, second_ref, second_out_ref):
    first_ref[...] = a_ref[0] + a_in_ref[0].astype(F32)
    second_ref[...] = b_ref[0] + b_in_ref[0].astype(F32)
    first_out_ref[...] = (a_ref[1] + a_in_ref[1].astype(F32)).astype(BF16)
    second_out_ref[...] = (b_ref[1] + b_in_ref[1].astype(F32)).astype(BF16)


def add_far(a_ref, a_in_ref, b_ref, b_in_ref, sum_ref, *out_refs):
    half = a_ref.shape[1]
    for far, out_ref in enumerate((sum_ref,) + out_refs):
        out_ref[0:half, :] = (a_ref[far] + a_in_ref[far].astype(F32)).astype(out_ref.dtype)
        out_ref[half:, :] = (b_ref[far] + b_in_ref[far].astype(F32)).astype(out_ref.dtype)


def local(
    devices,
    tile_forcing,
    elevation_gap,
    lapse_rate,
    column_tile,
    column_target,
    owner_counts,
    land_state,
    w_in,
    norm_gains,
    w_up,
    w_down,
    w_out,
):
    capacity, width = land_state.shape
    per_peer = capacity // devices + 1
    places = -(-per_peer // 128) * 128
    columns = elevation_gap.shape[0]
    tiles = tile_forcing.shape[0]
    guest_rows = -(-capacity // (2 * ROWS)) * ROWS
    meta_rows = -(-capacity // (8 * ROWS)) * 8
    bits = devices.bit_length() - 1
    me = lax.axis_index(AXES)

    def swap(values, bit):
        return lax.ppermute(values, AXES, [(i, i ^ bit) for i in range(devices)])

    small = pltpu.CompilerParams(vmem_limit_bytes=24 << 20)
    buckets, counts = pl.pallas_call(
        functools.partial(bucket_kernel, devices, capacity),
        out_shape=(
            jax.ShapeDtypeStruct((devices * FIELDS, places), BF16),
            jax.ShapeDtypeStruct((tiles, width), F32),
        ),
        in_specs=[VMEM] * 3,
        out_specs=(VMEM, VMEM),
        cost_estimate=cost(4.0),
        compiler_params=small,
        name="bucket",
    )(
        column_target.reshape(1, columns),
        column_tile.reshape(1, columns),
        elevation_gap.reshape(1, columns),
    )
    got = lax.all_to_all(
        buckets.reshape(devices, FIELDS, places), AXES, split_axis=0, concat_axis=0, tiled=True
    )
    tile_forcing, counts, mine = lax.optimization_barrier((tile_forcing, counts, owner_counts))

    far = 1 << (bits - 3)
    half = tiles // 2
    gathered = [tile_forcing] + [swap(tile_forcing, s << 3) for s in range(1, far)]
    first = jnp.stack([piece[:half] for piece in gathered])
    second = jnp.stack([piece[half:] for piece in gathered])
    first = jnp.stack([first, swap(first, 2)])
    second = jnp.stack([second, swap(second, 4)])
    first = jnp.stack([first, swap(first, 4)])
    second = jnp.stack([second, swap(second, 2)], axis=1)
    groups = devices // 2
    even = jnp.stack([first, second]).reshape(groups * tiles, width)
    odd = swap(even, 1)

    other_count = swap(mine, 1)
    guest_state = swap(land_state[:guest_rows].astype(BF16), 1)

    mine, theirs = pl.pallas_call(
        functools.partial(arrange_kernel, devices, tiles),
        out_shape=(jax.ShapeDtypeStruct((2, meta_rows, ROWS), F32),) * 2,
        in_specs=[SMEM, VMEM],
        out_specs=(VMEM,) * 2,
        cost_estimate=cost(4.0),
        compiler_params=small,
        name="arrange",
    )(me.astype(jnp.int32)[None], got.reshape(devices * FIELDS, places))
    guest_mine = swap(theirs, 1)
    table_rows = devices * tiles
    network_bytes = (
        (12 << 20)
        + (capacity + guest_rows) * width * 8
        + (w_in.size + w_up.size + w_down.size + w_out.size) * 2
        + table_rows * width * 18
    )
    network_bytes = min(network_bytes, 60 * 1024 * 1024)
    tend, guest_tend, keep, send = pl.pallas_call(
        network_kernel,
        out_shape=(
            jax.ShapeDtypeStruct((capacity, width), BF16),
            jax.ShapeDtypeStruct((guest_rows, width), BF16),
            jax.ShapeDtypeStruct((groups * tiles, width), F32),
            jax.ShapeDtypeStruct((groups * tiles, width), BF16),
        ),
        in_specs=[SMEM] * 2 + [VMEM] * 12,
        out_specs=(VMEM,) * 4,
        scratch_shapes=[
            pltpu.VMEM((table_rows + 8, width), F32),
            pltpu.VMEM((table_rows + 8, width), F32),
            pltpu.VMEM((table_rows + 8, width), F32),
            pltpu.VMEM((2 * ROWS, width), F32),
            pltpu.VMEM((2 * ROWS, width), F32),
            pltpu.VMEM((2, ROWS, width), BF16),
            pltpu.VMEM((2, 8, ROWS), F32),
            pltpu.VMEM((2 * meta_rows + 8, ROWS), jnp.int32),
            pltpu.SMEM((2 * meta_rows + 8, ROWS), jnp.int32),
            pltpu.SemaphoreType.DMA,
        ],
        cost_estimate=cost(50.0),
        compiler_params=pltpu.CompilerParams(vmem_limit_bytes=network_bytes),
        name="network",
    )(
        owner_counts,
        other_count,
        land_state,
        guest_state,
        mine,
        guest_mine,
        even,
        odd,
        lapse_rate.reshape(1, width),
        w_in,
        norm_gains,
        w_up[0],
        w_down[0],
        w_out,
    )
    back = swap(guest_tend, 1)

    def add(kernel, shapes, *arrays):
        return pl.pallas_call(
            kernel,
            out_shape=tuple(jax.ShapeDtypeStruct(shape, dtype) for shape, dtype in shapes),
            in_specs=[VMEM] * len(arrays),
            out_specs=(VMEM,) * len(shapes),
            cost_estimate=cost(0.5),
            compiler_params=small,
            name="add",
        )(*arrays)

    shape = (2, 2, 2, far, half, width)
    block = (2, far, half, width)
    first, first_out, second, second_out = add(
        add_near, [(block, F32), (block, BF16)] * 2, keep.reshape(shape), swap(send.reshape(shape), 1)
    )
    block = (far, half, width)
    first, first_out, second, second_out = add(
        add_next,
        [(block, F32), (block, BF16)] * 2,
        first,
        swap(first_out, 2),
        second,
        swap(second_out, 4),
    )
    block = (tiles, width)
    sums, *parts = add(
        add_far,
        [(block, F32)] + [(block, BF16)] * (far - 1),
        first,
        swap(first_out, 4),
        second,
        swap(second_out, 2),
    )
    parts = [swap(part, s << 3) for s, part in zip(range(1, far), parts)]
    for part in parts:
        sums = sums + part.astype(F32)
    tile_flux = sums / jnp.maximum(counts, 1.0)

    slot = jnp.arange(capacity, dtype=jnp.int32)[:, None]
    given, _ = tile_ranges(owner_counts[0], other_count[0])
    padded = jnp.pad(back, ((0, capacity - guest_rows), (0, 0)))
    change = jnp.where(slot < given * ROWS, padded, tend).astype(F32)
    new_state = jnp.where(slot < owner_counts[0], land_state + change, jnp.float32(0.0))
    return (new_state, tile_flux)


def solution(mesh):
    devices = mesh.shape["atm"] * mesh.shape["land"]
    rows, whole = P(AXES, None), P()

    def body(*arrays):
        return local(devices, *arrays)

    return jax.shard_map(
        body,
        mesh=mesh,
        in_specs=(rows, P(AXES), whole, P(AXES), P(AXES), P(AXES), rows) + (whole,) * 5,
        out_specs=(rows, rows),
        check_vma=False,
    )
```

profile of v0, /device:TPU:0, one launch (start us, length us, event | category | flops | bytes accessed | tf_op | source)
XLA Modules:
  0.0 107.8 jit_solution(4079151156533123060)
XLA Ops:
  0.6 0.0 copy-start.8
  0.6 0.7 copy-done.8
  1.3 0.7 copy-done.9
  2.0 0.7 copy-done.10
  2.7 1.6 %bucket.1 = (bf16[256,256]{1,0:T(8,128)(2,1)}, f32[128,128]{1,0:T(8,128)S(1)}) custom-call(s32[1,2048]{1,0:T(1,128)S(1)} %bitcast.58, s32[1,2048]{1,0:T(1,128)S(1)} %bitcast.59, f32[1,2048]{1,0:T(1,128)S(1)} %bitcast.60), custom_call_target="tpu_custom_call" | custom-call | flops 32000000 | bytes 8000000 | tf_op jit(solution)/shard_map/bucket/pallas_call | solution.py:317
  4.3 3.1 %collective-permute-start.3 = (bf16[128,128]{1,0:T(8,128)(2,1)}, bf16[128,128]{1,0:T(8,128)(2,1)S(1)}, u32[]{:S(2)}, u32[]{:S(2)}) collective-permute-start(bf16[128,128]{1,0:T(8,128)(2,1)} %param.12), channel_id=1, source_target_pairs={{0,8},{1,9},{2,10},{3,11},{4,12},{5,13},{6,14},{7,15},{8,0},{9,1},... | collective-permute-start | bytes 98312 | tf_op jit(solution)/shard_map/ppermute | solution.py:314
  7.4 2.6 %collective-permute-start.4 = (bf16[128,128]{1,0:T(8,128)(2,1)}, bf16[128,128]{1,0:T(8,128)(2,1)S(1)}, u32[]{:S(2)}, u32[]{:S(2)}) collective-permute-start(bf16[128,128]{1,0:T(8,128)(2,1)} %param.12), channel_id=1, source_target_pairs={{0,16},{1,17},{2,18},{3,19},{4,20},{5,21},{6,22},{7,23},{8,24},{9,... | collective-permute-start | bytes 98312 | tf_op jit(solution)/shard_map/ppermute | solution.py:314
  9.9 0.0 collective-permute-start.5
  10.0 0.8 slice_bitcast_fusion.7
  10.7 0.0 collective-permute-done.3
  10.7 2.2 %collective-permute-done.4 = bf16[128,128]{1,0:T(8,128)(2,1)S(1)} collective-permute-done((bf16[128,128]{1,0:T(8,128)(2,1)}, bf16[128,128]{1,0:T(8,128)(2,1)S(1)}, u32[]{:S(2)}, u32[]{:S(2)}) %collective-permute-start.4) | collective-permute-done | bytes 32800 | tf_op jit(solution)/shard_map/ppermute | solution.py:314
  13.0 2.9 %collective-permute-done.5 = bf16[128,128]{1,0:T(8,128)(2,1)S(1)} collective-permute-done((bf16[128,128]{1,0:T(8,128)(2,1)}, bf16[128,128]{1,0:T(8,128)(2,1)S(1)}, u32[]{:S(2)}, u32[]{:S(2)}) %collective-permute-start.5) | collective-permute-done | bytes 32800 | tf_op jit(solution)/shard_map/ppermute | solution.py:314
  15.9 1.6 %collective-permute-start.6 = (bf16[4,64,128]{2,1,0:T(8,128)(2,1)S(1)}, bf16[4,64,128]{2,1,0:T(8,128)(2,1)S(1)}, u32[]{:S(2)}, u32[]{:S(2)}) collective-permute-start(bf16[4,64,128]{2,1,0:T(8,128)(2,1)S(1)} %get-tuple-element.53), channel_id=1, source_target_pairs={{0,2},{1,3},{2,0},{3,1},{4,6},{5,7},{6,4},{7,5},{8,10},{9,11},{10,... | collective-permute-start | bytes 196616 | tf_op jit(solution)/shard_map/ppermute | solution.py:314
  17.5 1.6 %collective-permute-start.8 = (bf16[4,64,128]{2,1,0:T(8,128)(2,1)S(1)}, bf16[4,64,128]{2,1,0:T(8,128)(2,1)S(1)}, u32[]{:S(2)}, u32[]{:S(2)}) collective-permute-start(bf16[4,64,128]{2,1,0:T(8,128)(2,1)S(1)} %get-tuple-element.55), channel_id=1, source_target_pairs={{0,4},{1,5},{2,6},{3,7},{4,0},{5,1},{6,2},{7,3},{8,12},{9,13},{10,... | collective-permute-start | bytes 196616 | tf_op jit(solution)/shard_map/ppermute | solution.py:314
  19.1 1.2 %collective-permute-done.6 = bf16[4,64,128]{2,1,0:T(8,128)(2,1)S(1)} collective-permute-done((bf16[4,64,128]{2,1,0:T(8,128)(2,1)S(1)}, bf16[4,64,128]{2,1,0:T(8,128)(2,1)S(1)}, u32[]{:S(2)}, u32[]{:S(2)}) %collective-permute-start.6) | collective-permute-done | bytes 65568 | tf_op jit(solution)/shard_map/ppermute | solution.py:314
  20.2 1.6 %collective-permute-start.7 = (bf16[2,4,64,128]{3,2,1,0:T(8,128)(2,1)S(1)}, bf16[2,4,64,128]{3,2,1,0:T(8,128)(2,1)S(1)}, u32[]{:S(2)}, u32[]{:S(2)}) collective-permute-start(bf16[2,4,64,128]{3,2,1,0:T(8,128)(2,1)S(1)} %get-tuple-element.49), channel_id=1, source_target_pairs={{0,4},{1,5},{2,6},{3,7},{4,0},{5,1},{6,2},{7,3},{8,12},{9,13},{10,... | collective-permute-start | bytes 393224 | tf_op jit(solution)/shard_map/ppermute | solution.py:314
  21.8 0.3 collective-permute-done.8
  22.1 1.3 %collective-permute-start.9 = (bf16[2,4,64,128]{3,2,1,0:T(8,128)(2,1)S(1)}, bf16[2,4,64,128]{3,2,1,0:T(8,128)(2,1)S(1)}, u32[]{:S(2)}, u32[]{:S(2)}) collective-permute-start(bf16[2,4,64,128]{3,2,1,0:T(8,128)(2,1)S(1)} %get-tuple-element.51), channel_id=1, source_target_pairs={{0,2},{1,3},{2,0},{3,1},{4,6},{5,7},{6,4},{7,5},{8,10},{9,11},{10,... | collective-permute-start | bytes 393224 | tf_op jit(solution)/shard_map/ppermute | solution.py:314
  23.4 2.2 %slice.53 = bf16[2560,128]{1,0:T(8,128)(2,1)} slice(f32[5120,128]{1,0:T(8,128)} %state_ref.1), slice={[0:2560], [0:128]} | slice | bytes 1310720 | tf_op jit(solution)/shard_map/slice | solution.py:352
  25.6 0.0 collective-permute-start.1
  25.7 0.0 collective-permute-done.7
  25.7 1.5 %collective-permute-done.9 = bf16[2,4,64,128]{3,2,1,0:T(8,128)(2,1)S(1)} collective-permute-done((bf16[2,4,64,128]{3,2,1,0:T(8,128)(2,1)S(1)}, bf16[2,4,64,128]{3,2,1,0:T(8,128)(2,1)S(1)}, u32[]{:S(2)}, u32[]{:S(2)}) %collective-permute-start.9) | collective-permute-done | bytes 131104 | tf_op jit(solution)/shard_map/ppermute | solution.py:314
  27.2 0.1 pad_maximum_fusion
  27.3 0.1 collective-permute-start.10
  27.4 2.6 %all-to-all-start = ((bf16[32,8,256]{2,1,0:T(8,128)(2,1)}), bf16[32,8,256]{2,1,0:T(8,128)(2,1)S(1)}, u32[]{:S(2)}, u32[]{:S(2)}) async-start(bf16[32,8,256]{2,1,0:T(8,128)(2,1)} %bitcast.6), calls=%async_computation | async-start | bytes 262144 | tf_op jit(solution)/shard_map/all_to_all | solution.py:333
  30.0 8.2 %all-to-all-done = bf16[32,8,256]{2,1,0:T(8,128)(2,1)S(1)} async-done(((bf16[32,8,256]{2,1,0:T(8,128)(2,1)}), bf16[32,8,256]{2,1,0:T(8,128)(2,1)S(1)}, u32[]{:S(2)}, u32[]{:S(2)}) %all-to-all-start) | async-done | bytes 131104 | tf_op jit(solution)/shard_map/all_to_all | solution.py:333
  38.2 1.5 %arrange.1 = (f32[2,24,256]{2,1,0:T(8,128)S(1)}, f32[2,24,256]{2,1,0:T(8,128)S(1)}) custom-call(s32[1]{0:T(128)} %bitcast.5.me_ref, bf16[256,256]{1,0:T(8,128)(2,1)S(1)} %bitcast.55), custom_call_target="tpu_custom_call" | custom-call | flops 32000000 | bytes 8000000 | tf_op jit(solution)/shard_map/arrange/pallas_call | solution.py:354
  39.7 0.3 collective-permute-start.2
  40.0 0.3 collective-permute-start
  40.9 0.5 collective-permute-done.other_ref
  41.4 0.0 collective-permute-done.2.guest_mine_ref
  41.4 0.0 collective-permute-done.1.guest_ref
  41.4 0.0 collective-permute-done.10.odd_ref
  41.4 0.0 copy-done
  41.4 0.0 copy-done.6
  41.4 0.0 copy-done.7
  41.4 0.0 copy-start.1
  41.4 1.6 %copy-done.1 = bf16[1,1024,1024]{2,1,0:T(8,128)(2,1)S(1)} copy-done((bf16[1,1024,1024]{2,1,0:T(8,128)(2,1)S(1)}, bf16[1,1024,1024]{2,1,0:T(8,128)(2,1)}, u32[]{:S(2)}) %copy-start.1) | copy-done | bytes 2097176
  43.0 1.6 %copy-done.2 = bf16[1,1024,1024]{2,1,0:T(8,128)(2,1)S(1)} copy-done((bf16[1,1024,1024]{2,1,0:T(8,128)(2,1)S(1)}, bf16[1,1024,1024]{2,1,0:T(8,128)(2,1)}, u32[]{:S(2)}) %copy-start.2) | copy-done | bytes 2097176
  44.6 1.0 copy-done.4
  45.7 1.0 copy-done.5
  46.7 34.1 %network.1 = (bf16[5120,128]{1,0:T(8,128)(2,1)S(1)}, bf16[2560,128]{1,0:T(8,128)(2,1)}, f32[2048,128]{1,0:T(8,128)S(1)}, bf16[2048,128]{1,0:T(8,128)(2,1)S(1)}) custom-call(s32[1]{0:T(128)} %copy.16.own_ref, s32[1]{0:T(128)} %collective-permute-done.other_ref, f32[5120,128]{1,0:T(8,128)S(1)} %copy-done, bf16[2560,128]{1,0:T(8,128)(2,1)} %collective-permute-done.1.guest_ref, ...), custom_call_target="tpu_custom_call" | custom-call | flops 400000000 | bytes 100000000 | tf_op jit(solution)/shard_map/network/pallas_call | solution.py:372
  80.8 1.1 %copy-done.3 = bf16[5120,128]{1,0:T(8,128)(2,1)} copy-done((bf16[5120,128]{1,0:T(8,128)(2,1)}, bf16[5120,128]{1,0:T(8,128)(2,1)S(1)}, u32[]{:S(2)}) %copy-start.3) | copy-done | bytes 1310744
  81.9 0.0 collective-permute-start.12
  81.9 0.5 collective-permute-start.11
  82.4 1.4 %collective-permute-done.12.in_ref = bf16[2,2,2,4,64,128]{5,4,3,2,1,0:T(8,128)(2,1)S(1)} collective-permute-done((bf16[2,2,2,4,64,128]{5,4,3,2,1,0:T(8,128)(2,1)S(1)}, bf16[2,2,2,4,64,128]{5,4,3,2,1,0:T(8,128)(2,1)S(1)}, u32[]{:S(2)}, u32[]{:S(2)}) %collective-permute-start.12) | collective-permute-done | bytes 524320 | tf_op jit(solution)/shard_map/ppermute | solution.py:314
  83.8 0.8 add.30
  84.6 0.0 collective-permute-start.13
  84.6 0.6 collective-permute-start.14
  85.8 4.5 %collective-permute-done.13.a_in_ref = bf16[2,4,64,128]{3,2,1,0:T(8,128)(2,1)S(1)} collective-permute-done((bf16[2,4,64,128]{3,2,1,0:T(8,128)(2,1)}, bf16[2,4,64,128]{3,2,1,0:T(8,128)(2,1)S(1)}, u32[]{:S(2)}, u32[]{:S(2)}) %collective-permute-start.13) | collective-permute-done | bytes 131104 | tf_op jit(solution)/shard_map/ppermute | solution.py:314
  90.3 0.0 collective-permute-done.14.b_in_ref
  90.4 0.6 collective-permute-start.15
  91.0 1.7 %collective-permute-start.16 = (bf16[4,64,128]{2,1,0:T(8,128)(2,1)S(1)}, bf16[4,64,128]{2,1,0:T(8,128)(2,1)S(1)}, u32[]{:S(2)}, u32[]{:S(2)}) collective-permute-start(bf16[4,64,128]{2,1,0:T(8,128)(2,1)S(1)} %get-tuple-element.42), channel_id=1, source_target_pairs={{0,2},{1,3},{2,0},{3,1},{4,6},{5,7},{6,4},{7,5},{8,10},{9,11},{10,... | collective-permute-start | bytes 196616 | tf_op jit(solution)/shard_map/ppermute | solution.py:314
  92.7 2.0 %collective-permute-done.15.a_in_ref = bf16[4,64,128]{2,1,0:T(8,128)(2,1)S(1)} collective-permute-done((bf16[4,64,128]{2,1,0:T(8,128)(2,1)S(1)}, bf16[4,64,128]{2,1,0:T(8,128)(2,1)S(1)}, u32[]{:S(2)}, u32[]{:S(2)}) %collective-permute-start.15) | collective-permute-done | bytes 65568 | tf_op jit(solution)/shard_map/ppermute | solution.py:314
  94.7 0.6 collective-permute-done.16.b_in_ref
  95.3 0.8 collective-permute-start.17
  96.0 0.0 collective-permute-start.18
  96.1 3.7 %collective-permute-start.19 = (bf16[128,128]{1,0:T(8,128)(2,1)S(1)}, bf16[128,128]{1,0:T(8,128)(2,1)S(1)}, u32[]{:S(2)}, u32[]{:S(2)}) collective-permute-start(bf16[128,128]{1,0:T(8,128)(2,1)S(1)} %get-tuple-element.46), channel_id=1, source_target_pairs={{0,24},{1,25},{2,26},{3,27},{4,28},{5,29},{6,30},{7,31},{8,16},{9,... | collective-permute-start | bytes 98312 | tf_op jit(solution)/shard_map/ppermute | solution.py:314
  99.7 0.0 collective-permute-done.11
  99.7 7.4 %add_select_fusion = f32[5120,128]{1,0:T(8,128)} fusion(f32[5120,128]{1,0:T(8,128)S(1)} %copy-done, bf16[5120,128]{1,0:T(8,128)(2,1)} %copy-done.3, bf16[2560,128]{1,0:T(8,128)(2,1)} %collective-permute-done.11, pred[5120]{0:T(1024)(128)(4,1)S(1)} %iota_compare_fusion, pred[5120]{0:T(1024)(128)(4,1)S(1)} %iota_compare_fusion.1), kind=kLoop, calls=%fused_computation | loop fusion | flops 2621440 | bytes 7219200 | tf_op jit(solution)/shard_map/jit(_where)/select_n | solution.py:458
  107.2 0.0 collective-permute-done.17
  107.2 0.0 collective-permute-done.18
  107.2 0.0 collective-permute-done.19
  107.2 0.7 maximum_divide_fusion
  (23 shorter events, 0.3 us)
Async XLA Ops:
  0.6 0.7 copy-start.8
  1.3 0.7 copy-start.9
  2.0 0.7 copy-start.10
  4.3 6.4 %collective-permute-start.3 = (bf16[128,128]{1,0:T(8,128)(2,1)}, bf16[128,128]{1,0:T(8,128)(2,1)S(1)}, u32[]{:S(2)}, u32[]{:S(2)}) collective-permute-start(bf16[128,128]{1,0:T(8,128)(2,1)} %param.12), channel_id=1, source_target_pairs={{0,8},{1,9},{2,10},{3,11},{4,12},{5,13},{6,14},{7,15},{8,0},{9,1},... | collective-permute-start | bytes 98312 | tf_op jit(solution)/shard_map/ppermute | solution.py:314
  7.4 5.6 %collective-permute-start.4 = (bf16[128,128]{1,0:T(8,128)(2,1)}, bf16[128,128]{1,0:T(8,128)(2,1)S(1)}, u32[]{:S(2)}, u32[]{:S(2)}) collective-permute-start(bf16[128,128]{1,0:T(8,128)(2,1)} %param.12), channel_id=1, source_target_pairs={{0,16},{1,17},{2,18},{3,19},{4,20},{5,21},{6,22},{7,23},{8,24},{9,... | collective-permute-start | bytes 98312 | tf_op jit(solution)/shard_map/ppermute | solution.py:314
  9.9 5.9 %collective-permute-start.5 = (bf16[128,128]{1,0:T(8,128)(2,1)}, bf16[128,128]{1,0:T(8,128)(2,1)S(1)}, u32[]{:S(2)}, u32[]{:S(2)}) collective-permute-start(bf16[128,128]{1,0:T(8,128)(2,1)} %param.12), channel_id=1, source_target_pairs={{0,24},{1,25},{2,26},{3,27},{4,28},{5,29},{6,30},{7,31},{8,16},{9,... | collective-permute-start | bytes 98312 | tf_op jit(solution)/shard_map/ppermute | solution.py:314
  15.9 4.3 %collective-permute-start.6 = (bf16[4,64,128]{2,1,0:T(8,128)(2,1)S(1)}, bf16[4,64,128]{2,1,0:T(8,128)(2,1)S(1)}, u32[]{:S(2)}, u32[]{:S(2)}) collective-permute-start(bf16[4,64,128]{2,1,0:T(8,128)(2,1)S(1)} %get-tuple-element.53), channel_id=1, source_target_pairs={{0,2},{1,3},{2,0},{3,1},{4,6},{5,7},{6,4},{7,5},{8,10},{9,11},{10,... | collective-permute-start | bytes 196616 | tf_op jit(solution)/shard_map/ppermute | solution.py:314
  17.5 4.6 %collective-permute-start.8 = (bf16[4,64,128]{2,1,0:T(8,128)(2,1)S(1)}, bf16[4,64,128]{2,1,0:T(8,128)(2,1)S(1)}, u32[]{:S(2)}, u32[]{:S(2)}) collective-permute-start(bf16[4,64,128]{2,1,0:T(8,128)(2,1)S(1)} %get-tuple-element.55), channel_id=1, source_target_pairs={{0,4},{1,5},{2,6},{3,7},{4,0},{5,1},{6,2},{7,3},{8,12},{9,13},{10,... | collective-permute-start | bytes 196616 | tf_op jit(solution)/shard_map/ppermute | solution.py:314
  20.2 5.4 %collective-permute-start.7 = (bf16[2,4,64,128]{3,2,1,0:T(8,128)(2,1)S(1)}, bf16[2,4,64,128]{3,2,1,0:T(8,128)(2,1)S(1)}, u32[]{:S(2)}, u32[]{:S(2)}) collective-permute-start(bf16[2,4,64,128]{3,2,1,0:T(8,128)(2,1)S(1)} %get-tuple-element.49), channel_id=1, source_target_pairs={{0,4},{1,5},{2,6},{3,7},{4,0},{5,1},{6,2},{7,3},{8,12},{9,13},{10,... | collective-permute-start | bytes 393224 | tf_op jit(solution)/shard_map/ppermute | solution.py:314
  22.1 19.3 %copy-start = (f32[5120,128]{1,0:T(8,128)S(1)}, f32[5120,128]{1,0:T(8,128)}, u32[]{:S(2)}) copy-start(f32[5120,128]{1,0:T(8,128)} %state_ref.1) | copy-start | bytes 7864324
  22.1 19.3 %copy-start.6 = (f32[2,1024]{1,0:T(2,128)S(1)}, f32[2,1024]{1,0:T(2,128)}, u32[]{:S(2)}) copy-start(f32[2,1024]{1,0:T(2,128)} %gains_ref.1) | copy-start | bytes 24580
  22.1 19.3 %copy-start.7 = (f32[128]{0:T(128)S(1)}, f32[128]{0:T(128)}, u32[]{:S(2)}) copy-start(f32[128]{0:T(128)} %param.14) | copy-start | bytes 1540
  22.1 5.0 %collective-permute-start.9 = (bf16[2,4,64,128]{3,2,1,0:T(8,128)(2,1)S(1)}, bf16[2,4,64,128]{3,2,1,0:T(8,128)(2,1)S(1)}, u32[]{:S(2)}, u32[]{:S(2)}) collective-permute-start(bf16[2,4,64,128]{3,2,1,0:T(8,128)(2,1)S(1)} %get-tuple-element.51), channel_id=1, source_target_pairs={{0,2},{1,3},{2,0},{3,1},{4,6},{5,7},{6,4},{7,5},{8,10},{9,11},{10,... | collective-permute-start | bytes 393224 | tf_op jit(solution)/shard_map/ppermute | solution.py:314
  25.6 15.7 %collective-permute-start.1 = (bf16[2560,128]{1,0:T(8,128)(2,1)}, bf16[2560,128]{1,0:T(8,128)(2,1)}, u32[]{:S(2)}, u32[]{:S(2)}) collective-permute-start(bf16[2560,128]{1,0:T(8,128)(2,1)} %slice.53), channel_id=1, source_target_pairs={{0,1},{1,0},{2,3},{3,2},{4,5},{5,4},{6,7},{7,6},{8,9},{9,8},{10,11... | collective-permute-start | bytes 1966088 | tf_op jit(solution)/shard_map/ppermute | solution.py:314
  27.3 14.1 %collective-permute-start.10 = (bf16[2048,128]{1,0:T(8,128)(2,1)S(1)}, bf16[2048,128]{1,0:T(8,128)(2,1)}, u32[]{:S(2)}, u32[]{:S(2)}) collective-permute-start(bf16[2048,128]{1,0:T(8,128)(2,1)S(1)} %bitcast.50), channel_id=1, source_target_pairs={{0,1},{1,0},{2,3},{3,2},{4,5},{5,4},{6,7},{7,6},{8,9},{9,8},{10,11... | collective-permute-start | bytes 1572872 | tf_op jit(solution)/shard_map/ppermute | solution.py:314
  27.4 10.8 %all-to-all-start = ((bf16[32,8,256]{2,1,0:T(8,128)(2,1)}), bf16[32,8,256]{2,1,0:T(8,128)(2,1)S(1)}, u32[]{:S(2)}, u32[]{:S(2)}) async-start(bf16[32,8,256]{2,1,0:T(8,128)(2,1)} %bitcast.6), calls=%async_computation | async-start | bytes 262144 | tf_op jit(solution)/shard_map/all_to_all | solution.py:333
  39.7 1.7 %collective-permute-start.2 = (f32[2,24,256]{2,1,0:T(8,128)S(1)}, f32[2,24,256]{2,1,0:T(8,128)S(1)}, u32[]{:S(2)}, u32[]{:S(2)}) collective-permute-start(f32[2,24,256]{2,1,0:T(8,128)S(1)} %get-tuple-element.29), channel_id=1, source_target_pairs={{0,1},{1,0},{2,3},{3,2},{4,5},{5,4},{6,7},{7,6},{8,9},{9,8},{10,11... | collective-permute-start | bytes 147464 | tf_op jit(solution)/shard_map/ppermute | solution.py:314
  40.0 1.4 %collective-permute-start = (s32[1]{0:T(128)}, s32[1]{0:T(128)}, u32[]{:S(2)}, u32[]{:S(2)}) collective-permute-start(s32[1]{0:T(128)} %param.17), channel_id=1, source_target_pairs={{0,1},{1,0},{2,3},{3,2},{4,5},{5,4},{6,7},{7,6},{8,9},{9,8},{10,11... | collective-permute-start | bytes 20 | tf_op jit(solution)/shard_map/ppermute | solution.py:314
  41.4 1.6 %copy-start.1 = (bf16[1,1024,1024]{2,1,0:T(8,128)(2,1)S(1)}, bf16[1,1024,1024]{2,1,0:T(8,128)(2,1)}, u32[]{:S(2)}) copy-start(bf16[1,1024,1024]{2,1,0:T(8,128)(2,1)} %param.21) | copy-start | bytes 6291460
  43.0 1.6 %copy-start.2 = (bf16[1,1024,1024]{2,1,0:T(8,128)(2,1)S(1)}, bf16[1,1024,1024]{2,1,0:T(8,128)(2,1)}, u32[]{:S(2)}) copy-start(bf16[1,1024,1024]{2,1,0:T(8,128)(2,1)} %param.22) | copy-start | bytes 6291460
  44.6 1.0 copy-start.4
  45.7 1.0 copy-start.5
  80.8 1.1 %copy-start.3 = (bf16[5120,128]{1,0:T(8,128)(2,1)}, bf16[5120,128]{1,0:T(8,128)(2,1)S(1)}, u32[]{:S(2)}) copy-start(bf16[5120,128]{1,0:T(8,128)(2,1)S(1)} %get-tuple-element.32) | copy-start | bytes 3932164
  81.9 1.9 %collective-permute-start.12 = (bf16[2,2,2,4,64,128]{5,4,3,2,1,0:T(8,128)(2,1)S(1)}, bf16[2,2,2,4,64,128]{5,4,3,2,1,0:T(8,128)(2,1)S(1)}, u32[]{:S(2)}, u32[]{:S(2)}) collective-permute-start(bf16[2,2,2,4,64,128]{5,4,3,2,1,0:T(8,128)(2,1)S(1)} %bitcast.57), channel_id=1, source_target_pairs={{0,1},{1,0},{2,3},{3,2},{4,5},{5,4},{6,7},{7,6},{8,9},{9,8},{10,11... | collective-permute-start | bytes 1572872 | tf_op jit(solution)/shard_map/ppermute | solution.py:314
  81.9 17.9 %collective-permute-start.11 = (bf16[2560,128]{1,0:T(8,128)(2,1)}, bf16[2560,128]{1,0:T(8,128)(2,1)}, u32[]{:S(2)}, u32[]{:S(2)}) collective-permute-start(bf16[2560,128]{1,0:T(8,128)(2,1)} %get-tuple-element.31), channel_id=1, source_target_pairs={{0,1},{1,0},{2,3},{3,2},{4,5},{5,4},{6,7},{7,6},{8,9},{9,8},{10,11... | collective-permute-start | bytes 1966088 | tf_op jit(solution)/shard_map/ppermute | solution.py:314
  84.6 5.7 %collective-permute-start.13 = (bf16[2,4,64,128]{3,2,1,0:T(8,128)(2,1)}, bf16[2,4,64,128]{3,2,1,0:T(8,128)(2,1)S(1)}, u32[]{:S(2)}, u32[]{:S(2)}) collective-permute-start(bf16[2,4,64,128]{3,2,1,0:T(8,128)(2,1)} %get-tuple-element.36), channel_id=1, source_target_pairs={{0,2},{1,3},{2,0},{3,1},{4,6},{5,7},{6,4},{7,5},{8,10},{9,11},{10,... | collective-permute-start | bytes 393224 | tf_op jit(solution)/shard_map/ppermute | solution.py:314
  84.6 5.7 %collective-permute-start.14 = (bf16[2,4,64,128]{3,2,1,0:T(8,128)(2,1)}, bf16[2,4,64,128]{3,2,1,0:T(8,128)(2,1)S(1)}, u32[]{:S(2)}, u32[]{:S(2)}) collective-permute-start(bf16[2,4,64,128]{3,2,1,0:T(8,128)(2,1)} %get-tuple-element.38), channel_id=1, source_target_pairs={{0,4},{1,5},{2,6},{3,7},{4,0},{5,1},{6,2},{7,3},{8,12},{9,13},{10,... | collective-permute-start | bytes 393224 | tf_op jit(solution)/shard_map/ppermute | solution.py:314
  90.4 4.3 %collective-permute-start.15 = (bf16[4,64,128]{2,1,0:T(8,128)(2,1)S(1)}, bf16[4,64,128]{2,1,0:T(8,128)(2,1)S(1)}, u32[]{:S(2)}, u32[]{:S(2)}) collective-permute-start(bf16[4,64,128]{2,1,0:T(8,128)(2,1)S(1)} %get-tuple-element.40), channel_id=1, source_target_pairs={{0,4},{1,5},{2,6},{3,7},{4,0},{5,1},{6,2},{7,3},{8,12},{9,13},{10,... | collective-permute-start | bytes 196616 | tf_op jit(solution)/shard_map/ppermute | solution.py:314
  91.0 4.3 %collective-permute-start.16 = (bf16[4,64,128]{2,1,0:T(8,128)(2,1)S(1)}, bf16[4,64,128]{2,1,0:T(8,128)(2,1)S(1)}, u32[]{:S(2)}, u32[]{:S(2)}) collective-permute-start(bf16[4,64,128]{2,1,0:T(8,128)(2,1)S(1)} %get-tuple-element.42), channel_id=1, source_target_pairs={{0,2},{1,3},{2,0},{3,1},{4,6},{5,7},{6,4},{7,5},{8,10},{9,11},{10,... | collective-permute-start | bytes 196616 | tf_op jit(solution)/shard_map/ppermute | solution.py:314
  95.3 11.9 %collective-permute-start.17 = (bf16[128,128]{1,0:T(8,128)(2,1)S(1)}, bf16[128,128]{1,0:T(8,128)(2,1)S(1)}, u32[]{:S(2)}, u32[]{:S(2)}) collective-permute-start(bf16[128,128]{1,0:T(8,128)(2,1)S(1)} %get-tuple-element.44), channel_id=1, source_target_pairs={{0,8},{1,9},{2,10},{3,11},{4,12},{5,13},{6,14},{7,15},{8,0},{9,1},... | collective-permute-start | bytes 98312 | tf_op jit(solution)/shard_map/ppermute | solution.py:314
  96.0 11.1 %collective-permute-start.18 = (bf16[128,128]{1,0:T(8,128)(2,1)S(1)}, bf16[128,128]{1,0:T(8,128)(2,1)S(1)}, u32[]{:S(2)}, u32[]{:S(2)}) collective-permute-start(bf16[128,128]{1,0:T(8,128)(2,1)S(1)} %get-tuple-element.45), channel_id=1, source_target_pairs={{0,16},{1,17},{2,18},{3,19},{4,20},{5,21},{6,22},{7,23},{8,24},{9,... | collective-permute-start | bytes 98312 | tf_op jit(solution)/shard_map/ppermute | solution.py:314
  96.1 11.1 %collective-permute-start.19 = (bf16[128,128]{1,0:T(8,128)(2,1)S(1)}, bf16[128,128]{1,0:T(8,128)(2,1)S(1)}, u32[]{:S(2)}, u32[]{:S(2)}) collective-permute-start(bf16[128,128]{1,0:T(8,128)(2,1)S(1)} %get-tuple-element.46), channel_id=1, source_target_pairs={{0,24},{1,25},{2,26},{3,27},{4,28},{5,29},{6,30},{7,31},{8,16},{9,... | collective-permute-start | bytes 98312 | tf_op jit(solution)/shard_map/ppermute | solution.py:314
where the time goes:
time: 109 us; the launch traced here: 108 us
  Pallas kernels  38 us (35%)
  waiting for transfers between devices  25.2 us (23%)
  starting transfers between devices  22.8 us (21%)
  local copies, waits for them, and re-layouts  11.5 us (11%)
  other arithmetic  8.26 us (8%)
  between operations  2.1 us (2%)
    pallas_call x1, Pallas kernels, local(): pl.pallas_call(network_kernel, out_shape=(jax.ShapeDtypeStruct((capacity,...  34.1 us
    ppermute x20, starting transfers between devices, swap(): return lax.ppermute(values, AXES, [(i, i ^ bit) for i in range(devices)])  20.2 us
    ppermute x20, waiting for transfers between devices, swap(): return lax.ppermute(values, AXES, [(i, i ^ bit) for i in range(devices)])  17 us
    unnamed x22, local copies, waits for them, and re-layouts  8.47 us
    all_to_all x1, waiting for transfers between devices, local(): lax.all_to_all(buckets.reshape(devices, FIELDS, places), AXES, split_axis...  8.2 us
    select_n x1, other arithmetic, local(): jnp.where(slot < owner_counts[0], land_state + change, jnp.float32(0.0))  7.42 us
    all_to_all x1, starting transfers between devices, local(): lax.all_to_all(buckets.reshape(devices, FIELDS, places), AXES, split_axis...  2.59 us
    slice x1, local copies, waits for them, and re-layouts, local(): guest_state = swap(land_state[:guest_rows].astype(BF16), 1)  2.22 us
  transfers between devices with their start and end apart: 21, of which 11 were waited for; matrix products, arithmetic and copies ran while one was open for 10% of the time, Pallas kernels for 2%

commit v1 on v0

--- a/solution.py
+++ b/solution.py
@@ -13,6 +13,7 @@
 FIELDS = 8
 VMEM = pl.BlockSpec(memory_space=pltpu.VMEM)
 SMEM = pl.BlockSpec(memory_space=pltpu.SMEM)
+HBM = pl.BlockSpec(memory_space=pltpu.HBM)
 BF16 = jnp.bfloat16
 F32 = jnp.float32
 
@@ -23,6 +24,14 @@
 
 def dot_nt(a, b):
     return lax.dot_general(a, b, (((1,), (1,)), ((), ())), preferred_element_type=F32)
+
+
+def hbm(array):
+    return pltpu.with_memory_space_constraint(array, pltpu.HBM)
+
+
+def vmem(array):
+    return pltpu.with_memory_space_constraint(array, pltpu.VMEM)
 
 
 def cost(microseconds):
@@ -31,7 +40,25 @@
     )
 
 
-def bucket_kernel(devices, capacity, tgt_ref, tile_ref, gap_ref, out_ref, count_ref):
+def bucket_kernel(
+    devices,
+    capacity,
+    tgt_hbm,
+    tile_hbm,
+    gap_hbm,
+    out_ref,
+    count_ref,
+    tgt_ref,
+    tile_ref,
+    gap_ref,
+    sems,
+):
+    pairs = ((tgt_hbm, tgt_ref), (tile_hbm, tile_ref), (gap_hbm, gap_ref))
+    copies = [pltpu.make_async_copy(*pair, sems.at[place]) for place, pair in enumerate(pairs)]
+    for copy in copies:
+        copy.start()
+    for copy in copies:
+        copy.wait()
     columns = tgt_ref.shape[1]
     places = out_ref.shape[1]
     tiles = count_ref.shape[0]
@@ -83,7 +110,11 @@
     )
 
 
-def arrange_kernel(devices, tiles, me_ref, got_ref, mine_ref, guest_ref):
+def arrange_kernel(devices, tiles, me_ref, got_ref, weight_hbms, mine_ref, guest_ref, weight_refs, sems):
+    pairs = zip(weight_hbms, weight_refs)
+    copies = [pltpu.make_async_copy(*pair, sems.at[place]) for place, pair in enumerate(pairs)]
+    for copy in copies:
+        copy.start()
     places = got_ref.shape[1]
     rows = mine_ref.shape[1]
     total = jnp.zeros((5 * rows, ROWS), F32)
@@ -105,6 +136,8 @@
         row = table_row(devices, tiles, source ^ me, tile)
         out_ref[0] = jnp.where(source >= 0, row, devices * tiles).astype(F32)
         out_ref[1] = gap
+    for copy in copies:
+        copy.wait()
 
 
 def table_row(devices, tiles, relative, tile):
@@ -127,11 +160,11 @@
     guest_ref,
     mine_ref,
     guest_mine_ref,
-    even_ref,
-    odd_ref,
+    even_refs,
+    odd_refs,
     lapse_ref,
+    gains_ref,
     w_in_ref,
-    gains_ref,
     w_up_ref,
     w_down_ref,
     w_out_ref,
@@ -140,18 +173,18 @@
     keep_ref,
     send_ref,
     table_ref,
-    first_ref,
-    second_ref,
+    bank_refs,
     rows_ref,
     flux_ref,
     x_ref,
     gap_ref,
     index_ref,
     scalar_ref,
+    out_ref,
     sem,
+    out_sems,
 ):
-    half = even_ref.shape[0]
-    width = even_ref.shape[1]
+    half, width = keep_ref.shape
     spare = 2 * half
     given, have = tile_ranges(own_ref[0], other_ref[0])
     taken, _ = tile_ranges(other_ref[0], own_ref[0])
@@ -159,17 +192,30 @@
     all_tiles = own_tiles + taken
     lines = mine_ref.shape[1]
     last_line = 2 * lines
-
-    index_ref[0:lines, :] = mine_ref[0].astype(jnp.int32)
-    index_ref[lines:last_line, :] = guest_mine_ref[0].astype(jnp.int32)
-    index_ref[last_line:, :] = jnp.full_like(index_ref[last_line:, :], spare)
+    guest_rows = guest_ref.shape[0]
+    lanes = index_ref.shape[1]
+    parts = ROWS // lanes
+    part_lines = last_line + 8
+
+    for part in range(parts):
+        side = slice(part * lanes, (part + 1) * lanes)
+        base = part * part_lines
+        index_ref[base : base + lines, :] = mine_ref[0, :, side].astype(jnp.int32)
+        index_ref[base + lines : base + last_line, :] = guest_mine_ref[0, :, side].astype(jnp.int32)
+        index_ref[base + last_line : base + part_lines, :] = jnp.full((8, lanes), spare, jnp.int32)
     copy = pltpu.make_async_copy(index_ref, scalar_ref, sem)
     copy.start()
-    table_ref[0:half, :] = even_ref[...].astype(F32)
-    table_ref[half:spare, :] = odd_ref[...].astype(F32)
+    for core, pieces in enumerate((even_refs, odd_refs)):
+        base = core * half
+        run = pieces[0].shape[1] * pieces[0].shape[2]
+        for part, piece in enumerate(pieces):
+            for other in range(2):
+                y, x = (part % 2, other) if part < 2 else (other, part % 2)
+                at = base + (part // 2) * (half // 2) + (2 * y + x) * run
+                table_ref[at : at + run, :] = piece[other].astype(F32).reshape(run, width)
     table_ref[spare:, :] = jnp.zeros_like(table_ref[spare:, :])
-    first_ref[...] = jnp.zeros_like(first_ref)
-    second_ref[...] = jnp.zeros_like(second_ref)
+    for bank in bank_refs:
+        bank[...] = jnp.zeros_like(bank)
     copy.wait()
 
     def norm(values, gain):
@@ -192,15 +238,16 @@
             line = line_of(2 * step + chain)
             for row in range(ROWS):
                 at = chain * ROWS + row
-                rows_ref[at : at + 1, :] = table_ref[pl.ds(scalar_ref[line, row], 1), :]
+                where = scalar_ref[line + row // lanes * part_lines, row % lanes]
+                rows_ref[at : at + 1, :] = table_ref[pl.ds(where, 1), :]
 
     def spread(step):
         for chain in range(2):
             line = line_of(2 * step + chain)
             for row in range(ROWS):
                 at = chain * ROWS + row
-                bank = second_ref if row % 2 else first_ref
-                where = pl.ds(scalar_ref[line, row], 1)
+                bank = bank_refs[row % len(bank_refs)]
+                where = pl.ds(scalar_ref[line + row // lanes * part_lines, row % lanes], 1)
                 bank[where, :] = bank[where, :] + flux_ref[at : at + 1, :]
 
     def load(chain, step):
@@ -216,16 +263,32 @@
             x_ref[chain] = guest_ref[pl.ds(start, ROWS), :]
             gap_ref[chain] = jnp.broadcast_to(guest_mine_ref[1, pl.ds(index, 1), :], (8, ROWS))
 
-    def store(step, tend):
+    def store(chain, step, tend):
         is_own, _, start = place_of(step)
+        start = pl.multiple_of(jnp.where(step < all_tiles, start, guest_rows), ROWS)
+
+        @pl.when(step >= 2)
+        def _():
+            arrived(chain)
+
+        out_ref[chain] = tend
 
         @pl.when(is_own)
         def _():
-            tend_ref[pl.ds(start, ROWS), :] = tend
-
-        @pl.when(jnp.logical_not(is_own) & (step < all_tiles))
+            pltpu.make_async_copy(
+                out_ref.at[chain], tend_ref.at[pl.ds(start, ROWS)], out_sems.at[chain]
+            ).start()
+
+        @pl.when(jnp.logical_not(is_own))
         def _():
-            guest_tend_ref[pl.ds(start, ROWS), :] = tend
+            pltpu.make_async_copy(
+                out_ref.at[chain], guest_tend_ref.at[pl.ds(start, ROWS)], out_sems.at[chain]
+            ).start()
+
+    def arrived(chain):
+        pltpu.make_async_copy(
+            out_ref.at[chain], tend_ref.at[pl.ds(0, ROWS)], out_sems.at[chain]
+        ).wait()
 
     def two_tiles(step, _):
         chains = range(2)
@@ -252,15 +315,35 @@
                 result[chain][:, width:].astype(BF16).astype(F32)
             )
         for chain in chains:
-            store(2 * step + chain, result[chain][:, :width].astype(BF16))
+            store(chain, 2 * step + chain, result[chain][:, :width].astype(BF16))
         return 0
 
     steps = (all_tiles + 1) // 2
     fetch(0)
     lax.fori_loop(0, steps, two_tiles, 0)
     spread(steps - 1)
-    keep_ref[...] = first_ref[0:half, :] + second_ref[0:half, :]
-    send_ref[...] = (first_ref[half:spare, :] + second_ref[half:spare, :]).astype(BF16)
+    chunk = min(half, 128)
+
+    def gather(place, _):
+        low = pl.ds(pl.multiple_of(place * chunk, chunk), chunk)
+        high = pl.ds(pl.multiple_of(half + place * chunk, chunk), chunk)
+        keep_ref[low, :] = functools.reduce(jnp.add, [bank[low, :] for bank in bank_refs])
+        sums = functools.reduce(jnp.add, [bank[high, :] for bank in bank_refs])
+        send_ref[low, :] = sums.astype(BF16)
+        return 0
+
+    lax.fori_loop(0, half // chunk, gather, 0)
+    for chain in range(2):
+        arrived(chain)
+
+
+def finish_kernel(own_ref, other_ref, state_ref, tend_ref, back_ref, out_ref):
+    own = own_ref[0]
+    given, _ = tile_ranges(own, other_ref[0])
+    rows = out_ref.shape[0]
+    slot = iota((rows, 1), 0) + pl.program_id(0) * rows
+    change = jnp.where(slot < given * ROWS, back_ref[...].astype(F32), tend_ref[...].astype(F32))
+    out_ref[...] = jnp.where(slot < own, state_ref[...] + change, 0.0)
 
 
 def add_near(keep_ref, in_ref, first_ref, first_out_ref, second_ref, second_out_ref):
@@ -320,21 +403,25 @@
             jax.ShapeDtypeStruct((devices * FIELDS, places), BF16),
             jax.ShapeDtypeStruct((tiles, width), F32),
         ),
-        in_specs=[VMEM] * 3,
-        out_specs=(VMEM, VMEM),
-        cost_estimate=cost(4.0),
+        in_specs=[HBM] * 3,
+        out_specs=(VMEM,) * 2,
+        scratch_shapes=[
+            pltpu.VMEM((1, columns), jnp.int32),
+            pltpu.VMEM((1, columns), jnp.int32),
+            pltpu.VMEM((1, columns), F32),
+            pltpu.SemaphoreType.DMA((3,)),
+        ],
+        cost_estimate=cost(3.0),
         compiler_params=small,
         name="bucket",
     )(
-        column_target.reshape(1, columns),
-        column_tile.reshape(1, columns),
-        elevation_gap.reshape(1, columns),
+        hbm(column_target.reshape(1, columns)),
+        hbm(column_tile.reshape(1, columns)),
+        hbm(elevation_gap.reshape(1, columns)),
     )
     got = lax.all_to_all(
         buckets.reshape(devices, FIELDS, places), AXES, split_axis=0, concat_axis=0, tiled=True
     )
-    tile_forcing, counts, mine = lax.optimization_barrier((tile_forcing, counts, owner_counts))
-
     far = 1 << (bits - 3)
     half = tiles // 2
     gathered = [tile_forcing] + [swap(tile_forcing, s << 3) for s in range(1, far)]
@@ -342,54 +429,61 @@
     second = jnp.stack([piece[half:] for piece in gathered])
     first = jnp.stack([first, swap(first, 2)])
     second = jnp.stack([second, swap(second, 4)])
-    first = jnp.stack([first, swap(first, 4)])
-    second = jnp.stack([second, swap(second, 2)], axis=1)
+    even = (first, swap(first, 4), second, swap(second, 2))
     groups = devices // 2
-    even = jnp.stack([first, second]).reshape(groups * tiles, width)
-    odd = swap(even, 1)
-
-    other_count = swap(mine, 1)
+    odd = tuple(swap(piece, 1) for piece in even)
+
+    other_count = swap(owner_counts, 1)
     guest_state = swap(land_state[:guest_rows].astype(BF16), 1)
 
-    mine, theirs = pl.pallas_call(
+    weights = (w_in, w_up[0], w_down[0], w_out)
+    mine, theirs, weights = pl.pallas_call(
         functools.partial(arrange_kernel, devices, tiles),
-        out_shape=(jax.ShapeDtypeStruct((2, meta_rows, ROWS), F32),) * 2,
-        in_specs=[SMEM, VMEM],
-        out_specs=(VMEM,) * 2,
+        out_shape=(jax.ShapeDtypeStruct((2, meta_rows, ROWS), F32),) * 2
+        + (tuple(jax.ShapeDtypeStruct(w.shape, BF16) for w in weights),),
+        in_specs=[SMEM, VMEM, (HBM,) * 4],
+        out_specs=(VMEM, VMEM, (VMEM,) * 4),
+        scratch_shapes=[pltpu.SemaphoreType.DMA((4,))],
         cost_estimate=cost(4.0),
         compiler_params=small,
         name="arrange",
-    )(me.astype(jnp.int32)[None], got.reshape(devices * FIELDS, places))
+    )(
+        me.astype(jnp.int32)[None],
+        got.reshape(devices * FIELDS, places),
+        tuple(hbm(w) for w in weights),
+    )
     guest_mine = swap(theirs, 1)
     table_rows = devices * tiles
+    held = vmem if table_rows <= 8192 else hbm
     network_bytes = (
         (12 << 20)
         + (capacity + guest_rows) * width * 8
-        + (w_in.size + w_up.size + w_down.size + w_out.size) * 2
-        + table_rows * width * 18
-    )
-    network_bytes = min(network_bytes, 60 * 1024 * 1024)
+        + table_rows * width * (4 * (5 if table_rows <= 8192 else 2) + 10)
+    )
+    if table_rows > 8192:
+        network_bytes = 60 * 1024 * 1024
     tend, guest_tend, keep, send = pl.pallas_call(
         network_kernel,
         out_shape=(
             jax.ShapeDtypeStruct((capacity, width), BF16),
-            jax.ShapeDtypeStruct((guest_rows, width), BF16),
+            jax.ShapeDtypeStruct((guest_rows + ROWS, width), BF16),
             jax.ShapeDtypeStruct((groups * tiles, width), F32),
             jax.ShapeDtypeStruct((groups * tiles, width), BF16),
         ),
-        in_specs=[SMEM] * 2 + [VMEM] * 12,
-        out_specs=(VMEM,) * 4,
+        in_specs=[SMEM] * 2 + [VMEM] * 4 + [(VMEM,) * 4] * 2 + [VMEM] * 6,
+        out_specs=(HBM, HBM, VMEM, VMEM),
         scratch_shapes=[
             pltpu.VMEM((table_rows + 8, width), F32),
-            pltpu.VMEM((table_rows + 8, width), F32),
-            pltpu.VMEM((table_rows + 8, width), F32),
+            [pltpu.VMEM((table_rows + 8, width), F32)] * (4 if table_rows <= 8192 else 1),
             pltpu.VMEM((2 * ROWS, width), F32),
             pltpu.VMEM((2 * ROWS, width), F32),
             pltpu.VMEM((2, ROWS, width), BF16),
             pltpu.VMEM((2, 8, ROWS), F32),
-            pltpu.VMEM((2 * meta_rows + 8, ROWS), jnp.int32),
-            pltpu.SMEM((2 * meta_rows + 8, ROWS), jnp.int32),
+            pltpu.VMEM((ROWS // width * (2 * meta_rows + 8), width), jnp.int32),
+            pltpu.SMEM((ROWS // width * (2 * meta_rows + 8), width), jnp.int32),
+            pltpu.VMEM((2, ROWS, width), BF16),
             pltpu.SemaphoreType.DMA,
+            pltpu.SemaphoreType.DMA((2,)),
         ],
         cost_estimate=cost(50.0),
         compiler_params=pltpu.CompilerParams(vmem_limit_bytes=network_bytes),
@@ -401,14 +495,11 @@
         guest_state,
         mine,
         guest_mine,
-        even,
-        odd,
+        tuple(held(piece) for piece in even),
+        tuple(held(piece) for piece in odd),
         lapse_rate.reshape(1, width),
-        w_in,
         norm_gains,
-        w_up[0],
-        w_down[0],
-        w_out,
+        *(held(w) for w in weights),
     )
     back = swap(guest_tend, 1)
 
@@ -451,11 +542,19 @@
         sums = sums + part.astype(F32)
     tile_flux = sums / jnp.maximum(counts, 1.0)
 
-    slot = jnp.arange(capacity, dtype=jnp.int32)[:, None]
-    given, _ = tile_ranges(owner_counts[0], other_count[0])
-    padded = jnp.pad(back, ((0, capacity - guest_rows), (0, 0)))
-    change = jnp.where(slot < given * ROWS, padded, tend).astype(F32)
-    new_state = jnp.where(slot < owner_counts[0], land_state + change, jnp.float32(0.0))
+    part = guest_rows // 2
+    wide = pl.BlockSpec((part, width), lambda i: (i, 0))
+    new_state = pl.pallas_call(
+        finish_kernel,
+        out_shape=jax.ShapeDtypeStruct((capacity, width), F32),
+        grid=(-(-capacity // part),),
+        in_specs=[SMEM] * 2
+        + [wide, wide, pl.BlockSpec((part, width), lambda i: (jnp.minimum(i, 1), 0))],
+        out_specs=wide,
+        cost_estimate=cost(4.0),
+        compiler_params=small,
+        name="finish",
+    )(owner_counts, other_count, land_state, tend, back)
     return (new_state, tile_flux)
 
 

time: 109 us -> 87.5 us (0.80)
  waiting for transfers between devices: 25.2 us -> 13.4 us
  local copies, waits for them, and re-layouts: 11.5 us -> 2.15 us
  other arithmetic: 8.26 us -> 0.72 us
  starting transfers between devices: 22.8 us -> 28.6 us
  Pallas kernels: 38 us -> 40.7 us
    unnamed x22 -> x6, local copies, waits for them, and re-layouts: 8.47 us -> 0.02 us
    all_to_all x1, waiting for transfers between devices: 8.2 us -> 0.01 us  [local(): lax.all_to_all(buckets.reshape(devices, FIELDS, places), AXES, split_axis...]
    select_n x1 -> x0, other arithmetic: 7.42 us -> none  [local(): jnp.where(slot < owner_counts[0], land_state + change, jnp.float32(0.0))]
    ppermute x20 -> x23, waiting for transfers between devices: 17 us -> 13.3 us  [swap(): return lax.ppermute(values, AXES, [(i, i ^ bit) for i in range(devices)])]
    all_to_all x1, starting transfers between devices: 2.59 us -> 6.07 us  [local(): lax.all_to_all(buckets.reshape(devices, FIELDS, places), AXES, split_axis...]
    pallas_call x0 -> x1, Pallas kernels: none -> 2.94 us  [local(): pl.pallas_call(finish_kernel, out_shape=jax.ShapeDtypeStruct((capacity, w...]
    ppermute x20 -> x23, starting transfers between devices: 20.2 us -> 22.5 us  [swap(): return lax.ppermute(values, AXES, [(i, i ^ bit) for i in range(devices)])]
    pallas_call x1, Pallas kernels: 34.1 us -> 32.6 us  [local(): pl.pallas_call(network_kernel, out_shape=(jax.ShapeDtypeStruct((capacity,...]
  transfers between devices with their start and end apart: 21 -> 24, of which waited for: 11 -> 10; matrix products, arithmetic and copies ran while one was open for 10% -> 3% of each run, Pallas kernels for 2% -> 9%
where the time goes in v1:
time: 87.5 us; the launch traced here: 87 us
  Pallas kernels  40.7 us (47%)
  starting transfers between devices  28.6 us (33%)
  waiting for transfers between devices  13.4 us (15%)
  local copies, waits for them, and re-layouts  2.15 us (2%)
  between operations  1.47 us (2%)
    pallas_call x1, Pallas kernels, local(): pl.pallas_call(network_kernel, out_shape=(jax.ShapeDtypeStruct((capacity,...  32.6 us
    ppermute x23, starting transfers between devices, swap(): return lax.ppermute(values, AXES, [(i, i ^ bit) for i in range(devices)])  22.5 us
    ppermute x23, waiting for transfers between devices, swap(): return lax.ppermute(values, AXES, [(i, i ^ bit) for i in range(devices)])  13.3 us
    all_to_all x1, starting transfers between devices, local(): lax.all_to_all(buckets.reshape(devices, FIELDS, places), AXES, split_axis...  6.07 us
    pallas_call x1, Pallas kernels, local(): pl.pallas_call(finish_kernel, out_shape=jax.ShapeDtypeStruct((capacity, w...  2.94 us
    pallas_call x1, Pallas kernels, local(): pl.pallas_call(functools.partial(arrange_kernel, devices, tiles), out_sha...  2.65 us
    pallas_call x1, Pallas kernels, local(): pl.pallas_call(functools.partial(bucket_kernel, devices, capacity), out_s...  2.33 us
  transfers between devices with their start and end apart: 24, of which 10 were waited for; matrix products, arithmetic and copies ran while one was open for 3% of the time, Pallas kernels for 9%

profile of v1, /device:TPU:0, one launch (start us, length us, event | category | flops | bytes accessed | tf_op | source)
XLA Modules:
  0.0 87.0 jit_solution(1593724495637732206)
XLA Ops:
  0.6 3.1 %collective-permute-start.3 = (bf16[128,128]{1,0:T(8,128)(2,1)}, bf16[128,128]{1,0:T(8,128)(2,1)S(1)}, u32[]{:S(2)}, u32[]{:S(2)}) collective-permute-start(bf16[128,128]{1,0:T(8,128)(2,1)} %param.12), channel_id=1, source_target_pairs={{0,8},{1,9},{2,10},{3,11},{4,12},{5,13},{6,14},{7,15},{8,0},{9,1},... | collective-permute-start | bytes 98312 | tf_op jit(solution)/shard_map/ppermute | solution.py:397
  3.7 2.6 %collective-permute-start.4 = (bf16[128,128]{1,0:T(8,128)(2,1)}, bf16[128,128]{1,0:T(8,128)(2,1)S(1)}, u32[]{:S(2)}, u32[]{:S(2)}) collective-permute-start(bf16[128,128]{1,0:T(8,128)(2,1)} %param.12), channel_id=1, source_target_pairs={{0,16},{1,17},{2,18},{3,19},{4,20},{5,21},{6,22},{7,23},{8,24},{9,... | collective-permute-start | bytes 98312 | tf_op jit(solution)/shard_map/ppermute | solution.py:397
  6.3 0.0 collective-permute-start.5
  6.3 2.3 %bucket.1 = (bf16[256,256]{1,0:T(8,128)(2,1)}, f32[128,128]{1,0:T(8,128)S(1)}) custom-call(s32[1,2048]{1,0:T(1,128)} %bitcast.41, s32[1,2048]{1,0:T(1,128)} %bitcast.42, f32[1,2048]{1,0:T(1,128)} %bitcast.43), custom_call_target="tpu_custom_call" | custom-call | flops 24000000 | bytes 6000000 | tf_op jit(solution)/shard_map/bucket/pallas_call | solution.py:400
  8.7 6.1 %all-to-all-start = ((bf16[32,8,256]{2,1,0:T(8,128)(2,1)}), bf16[32,8,256]{2,1,0:T(8,128)(2,1)S(1)}, u32[]{:S(2)}, u32[]{:S(2)}) async-start(bf16[32,8,256]{2,1,0:T(8,128)(2,1)} %bitcast.4), calls=%async_computation | async-start | bytes 262144 | tf_op jit(solution)/shard_map/all_to_all | solution.py:422
  14.8 1.4 %slice.53 = bf16[2560,128]{1,0:T(8,128)(2,1)S(1)} slice(f32[5120,128]{1,0:T(8,128)} %state_ref.3), slice={[0:2560], [0:128]} | slice | bytes 1310720 | tf_op jit(solution)/shard_map/slice | solution.py:437
  16.1 0.3 collective-permute-start.1
  16.5 0.7 slice_bitcast_fusion.6
  17.2 0.0 collective-permute-done.3
  17.2 0.0 collective-permute-done.4
  17.2 0.0 collective-permute-done.5
  17.3 1.7 %collective-permute-start.6 = (bf16[4,64,128]{2,1,0:T(8,128)(2,1)S(1)}, bf16[4,64,128]{2,1,0:T(8,128)(2,1)S(1)}, u32[]{:S(2)}, u32[]{:S(2)}) collective-permute-start(bf16[4,64,128]{2,1,0:T(8,128)(2,1)S(1)} %get-tuple-element.53), channel_id=1, source_target_pairs={{0,2},{1,3},{2,0},{3,1},{4,6},{5,7},{6,4},{7,5},{8,10},{9,11},{10,... | collective-permute-start | bytes 196616 | tf_op jit(solution)/shard_map/ppermute | solution.py:397
  19.0 1.5 %collective-permute-start.8 = (bf16[4,64,128]{2,1,0:T(8,128)(2,1)S(1)}, bf16[4,64,128]{2,1,0:T(8,128)(2,1)S(1)}, u32[]{:S(2)}, u32[]{:S(2)}) collective-permute-start(bf16[4,64,128]{2,1,0:T(8,128)(2,1)S(1)} %get-tuple-element.51), channel_id=1, source_target_pairs={{0,4},{1,5},{2,6},{3,7},{4,0},{5,1},{6,2},{7,3},{8,12},{9,13},{10,... | collective-permute-start | bytes 196616 | tf_op jit(solution)/shard_map/ppermute | solution.py:397
  20.5 1.5 %collective-permute-done.6 = bf16[4,64,128]{2,1,0:T(8,128)(2,1)S(1)} collective-permute-done((bf16[4,64,128]{2,1,0:T(8,128)(2,1)S(1)}, bf16[4,64,128]{2,1,0:T(8,128)(2,1)S(1)}, u32[]{:S(2)}, u32[]{:S(2)}) %collective-permute-start.6) | collective-permute-done | bytes 65568 | tf_op jit(solution)/shard_map/ppermute | solution.py:397
  22.1 1.8 %collective-permute-start.7 = (bf16[2,4,64,128]{3,2,1,0:T(8,128)(2,1)S(1)}, bf16[2,4,64,128]{3,2,1,0:T(8,128)(2,1)S(1)}, u32[]{:S(2)}, u32[]{:S(2)}) collective-permute-start(bf16[2,4,64,128]{3,2,1,0:T(8,128)(2,1)S(1)} %pad_maximum_fusion.even_refs_0_), channel_id=1, source_target_pairs={{0,4},{1,5},{2,6},{3,7},{4,0},{5,1},{6,2},{7,3},{8,12},{9,13},{10,... | collective-permute-start | bytes 393224 | tf_op jit(solution)/shard_map/ppermute | solution.py:397
  23.8 0.0 collective-permute-done.8
  23.9 1.2 %collective-permute-start.9 = (bf16[2,4,64,128]{3,2,1,0:T(8,128)(2,1)S(1)}, bf16[2,4,64,128]{3,2,1,0:T(8,128)(2,1)S(1)}, u32[]{:S(2)}, u32[]{:S(2)}) collective-permute-start(bf16[2,4,64,128]{3,2,1,0:T(8,128)(2,1)S(1)} %pad_maximum_fusion.1.even_refs_2_), channel_id=1, source_target_pairs={{0,2},{1,3},{2,0},{3,1},{4,6},{5,7},{6,4},{7,5},{8,10},{9,11},{10,... | collective-permute-start | bytes 393224 | tf_op jit(solution)/shard_map/ppermute | solution.py:397
  25.1 0.0 collective-permute-start.10
  25.1 0.5 collective-permute-start
  25.6 1.1 %collective-permute-done.other_ref = s32[1]{0:T(128)} collective-permute-done((s32[1]{0:T(128)}, s32[1]{0:T(128)}, u32[]{:S(2)}, u32[]{:S(2)}) %collective-permute-start) | collective-permute-done | bytes 36 | tf_op jit(solution)/shard_map/ppermute | solution.py:397
  26.7 0.3 collective-permute-start.12
  27.0 0.1 collective-permute-done.7.even_refs_1_
  27.2 0.0 collective-permute-start.11
  27.2 1.7 %collective-permute-done.9.even_refs_3_ = bf16[2,4,64,128]{3,2,1,0:T(8,128)(2,1)S(1)} collective-permute-done((bf16[2,4,64,128]{3,2,1,0:T(8,128)(2,1)S(1)}, bf16[2,4,64,128]{3,2,1,0:T(8,128)(2,1)S(1)}, u32[]{:S(2)}, u32[]{:S(2)}) %collective-permute-start.9) | collective-permute-done | bytes 131104 | tf_op jit(solution)/shard_map/ppermute | solution.py:397
  28.9 0.0 collective-permute-start.13
  28.9 0.0 all-to-all-done
  28.9 0.0 copy-start
  28.9 0.0 copy-start.1
  28.9 0.0 copy-start.2
  28.9 2.7 %arrange.1 = (f32[2,24,256]{2,1,0:T(8,128)S(1)}, f32[2,24,256]{2,1,0:T(8,128)S(1)}, bf16[256,1024]{1,0:T(8,128)(2,1)S(1)}, bf16[1024,1024]{1,0:T(8,128)(2,1)S(1)...) custom-call(s32[1]{0:T(128)} %bitcast.me_ref, bf16[256,256]{1,0:T(8,128)(2,1)S(1)} %bitcast.34, ...), custom_call_target="tpu_custom_call" | custom-call | flops 32000000 | bytes 8000000 | tf_op jit(solution)/shard_map/arrange/pallas_call | solution.py:440
  31.6 0.0 collective-permute-done.10.odd_refs_0_
  31.6 0.6 collective-permute-start.2
  32.8 0.0 collective-permute-done.12.odd_refs_2_
  32.8 0.2 collective-permute-done.2.guest_mine_ref
  33.0 0.0 collective-permute-done.11.odd_refs_1_
  33.0 0.0 collective-permute-done.13.odd_refs_3_
  33.1 0.0 collective-permute-done.1.guest_ref
  33.1 0.0 copy-done
  33.1 0.0 copy-done.1
  33.1 0.0 copy-done.2
  33.1 32.6 %network.1 = (bf16[5120,128]{1,0:T(8,128)(2,1)S(1)}, bf16[2816,128]{1,0:T(8,128)(2,1)S(1)}, f32[2048,128]{1,0:T(8,128)S(1)}, bf16[2048,128]{1,0:T(8,128)(2,1)S(1)}) custom-call(s32[1]{0:T(128)S(6)} %copy.14.own_ref, s32[1]{0:T(128)} %collective-permute-done.other_ref, f32[5120,128]{1,0:T(8,128)S(1)} %copy-done, ...), custom_call_target="tpu_custom_call" | custom-call | flops 400000000 | bytes 100000000 | tf_op jit(solution)/shard_map/network/pallas_call | solution.py:465
  65.7 0.3 collective-permute-start.15
  66.0 0.3 collective-permute-start.14
  66.3 1.4 %collective-permute-done.15.in_ref = bf16[2,2,2,4,64,128]{5,4,3,2,1,0:T(8,128)(2,1)S(1)} collective-permute-done((bf16[2,2,2,4,64,128]{5,4,3,2,1,0:T(8,128)(2,1)S(1)}, bf16[2,2,2,4,64,128]{5,4,3,2,1,0:T(8,128)(2,1)S(1)}, u32[]{:S(2)}, u32[]{:S(2)}) %collective-permute-start.15) | collective-permute-done | bytes 524320 | tf_op jit(solution)/shard_map/ppermute | solution.py:397
  67.7 0.1 add.22
  67.8 0.1 collective-permute-start.16
  67.9 1.1 %collective-permute-start.17 = (bf16[2,4,64,128]{3,2,1,0:T(8,128)(2,1)S(1)}, bf16[2,4,64,128]{3,2,1,0:T(8,128)(2,1)S(1)}, u32[]{:S(2)}, u32[]{:S(2)}) collective-permute-start(bf16[2,4,64,128]{3,2,1,0:T(8,128)(2,1)S(1)} %get-tuple-element.40), channel_id=1, source_target_pairs={{0,4},{1,5},{2,6},{3,7},{4,0},{5,1},{6,2},{7,3},{8,12},{9,13},{10,... | collective-permute-start | bytes 393224 | tf_op jit(solution)/shard_map/ppermute | solution.py:397
  68.9 4.6 %collective-permute-done.16.a_in_ref = bf16[2,4,64,128]{3,2,1,0:T(8,128)(2,1)S(1)} collective-permute-done((bf16[2,4,64,128]{3,2,1,0:T(8,128)(2,1)S(1)}, bf16[2,4,64,128]{3,2,1,0:T(8,128)(2,1)S(1)}, u32[]{:S(2)}, u32[]{:S(2)}) %collective-permute-start.16) | collective-permute-done | bytes 131104 | tf_op jit(solution)/shard_map/ppermute | solution.py:397
  73.5 0.1 collective-permute-done.17.b_in_ref
  73.6 1.0 %collective-permute-start.18 = (bf16[4,64,128]{2,1,0:T(8,128)(2,1)S(1)}, bf16[4,64,128]{2,1,0:T(8,128)(2,1)S(1)}, u32[]{:S(2)}, u32[]{:S(2)}) collective-permute-start(bf16[4,64,128]{2,1,0:T(8,128)(2,1)S(1)} %get-tuple-element.42), channel_id=1, source_target_pairs={{0,4},{1,5},{2,6},{3,7},{4,0},{5,1},{6,2},{7,3},{8,12},{9,13},{10,... | collective-permute-start | bytes 196616 | tf_op jit(solution)/shard_map/ppermute | solution.py:397
  74.6 1.7 %collective-permute-start.19 = (bf16[4,64,128]{2,1,0:T(8,128)(2,1)S(1)}, bf16[4,64,128]{2,1,0:T(8,128)(2,1)S(1)}, u32[]{:S(2)}, u32[]{:S(2)}) collective-permute-start(bf16[4,64,128]{2,1,0:T(8,128)(2,1)S(1)} %get-tuple-element.44), channel_id=1, source_target_pairs={{0,2},{1,3},{2,0},{3,1},{4,6},{5,7},{6,4},{7,5},{8,10},{9,11},{10,... | collective-permute-start | bytes 196616 | tf_op jit(solution)/shard_map/ppermute | solution.py:397
  76.3 1.7 %collective-permute-done.18.a_in_ref = bf16[4,64,128]{2,1,0:T(8,128)(2,1)S(1)} collective-permute-done((bf16[4,64,128]{2,1,0:T(8,128)(2,1)S(1)}, bf16[4,64,128]{2,1,0:T(8,128)(2,1)S(1)}, u32[]{:S(2)}, u32[]{:S(2)}) %collective-permute-start.18) | collective-permute-done | bytes 65568 | tf_op jit(solution)/shard_map/ppermute | solution.py:397
  78.0 0.9 %collective-permute-done.19.b_in_ref = bf16[4,64,128]{2,1,0:T(8,128)(2,1)S(1)} collective-permute-done((bf16[4,64,128]{2,1,0:T(8,128)(2,1)S(1)}, bf16[4,64,128]{2,1,0:T(8,128)(2,1)S(1)}, u32[]{:S(2)}, u32[]{:S(2)}) %collective-permute-start.19) | collective-permute-done | bytes 65568 | tf_op jit(solution)/shard_map/ppermute | solution.py:397
  78.9 1.5 %collective-permute-start.20 = (bf16[128,128]{1,0:T(8,128)(2,1)S(1)}, bf16[128,128]{1,0:T(8,128)(2,1)S(1)}, u32[]{:S(2)}, u32[]{:S(2)}) collective-permute-start(bf16[128,128]{1,0:T(8,128)(2,1)S(1)} %get-tuple-element.46), channel_id=1, source_target_pairs={{0,8},{1,9},{2,10},{3,11},{4,12},{5,13},{6,14},{7,15},{8,0},{9,1},... | collective-permute-start | bytes 98312 | tf_op jit(solution)/shard_map/ppermute | solution.py:397
  80.4 0.0 collective-permute-start.21
  80.4 2.9 %collective-permute-start.22 = (bf16[128,128]{1,0:T(8,128)(2,1)S(1)}, bf16[128,128]{1,0:T(8,128)(2,1)S(1)}, u32[]{:S(2)}, u32[]{:S(2)}) collective-permute-start(bf16[128,128]{1,0:T(8,128)(2,1)S(1)} %get-tuple-element.48), channel_id=1, source_target_pairs={{0,24},{1,25},{2,26},{3,27},{4,28},{5,29},{6,30},{7,31},{8,16},{9,... | collective-permute-start | bytes 98312 | tf_op jit(solution)/shard_map/ppermute | solution.py:397
  83.4 0.0 collective-permute-done.14.back_ref
  83.4 2.9 %finish.1 = f32[5120,128]{1,0:T(8,128)} custom-call(s32[1]{0:T(128)S(6)} %copy.14.own_ref, s32[1]{0:T(128)} %collective-permute-done.other_ref, f32[5120,128]{1,0:T(8,128)S(1)} %copy-done, bf16[5120,128]{1,0:T(8,128)(2,1)S(1)} %get-tuple-element.33.tend_ref, bf16[2816,128]{1,0:T(8,128)(2,1)S(1)} %collective-permute-done.14.back_ref), custom_call_target="tpu_custom_call" | custom-call | flops 32000000 | bytes 8000000 | tf_op jit(solution)/shard_map/finish/pallas_call | solution.py:547
  86.3 0.0 collective-permute-done.20
  86.3 0.0 collective-permute-done.21
  86.3 0.0 collective-permute-done.22
  86.3 0.7 maximum_divide_fusion
  (9 shorter events, 0.1 us)
Async XLA Ops:
  0.6 16.6 %collective-permute-start.3 = (bf16[128,128]{1,0:T(8,128)(2,1)}, bf16[128,128]{1,0:T(8,128)(2,1)S(1)}, u32[]{:S(2)}, u32[]{:S(2)}) collective-permute-start(bf16[128,128]{1,0:T(8,128)(2,1)} %param.12), channel_id=1, source_target_pairs={{0,8},{1,9},{2,10},{3,11},{4,12},{5,13},{6,14},{7,15},{8,0},{9,1},... | collective-permute-start | bytes 98312 | tf_op jit(solution)/shard_map/ppermute | solution.py:397
  3.7 13.5 %collective-permute-start.4 = (bf16[128,128]{1,0:T(8,128)(2,1)}, bf16[128,128]{1,0:T(8,128)(2,1)S(1)}, u32[]{:S(2)}, u32[]{:S(2)}) collective-permute-start(bf16[128,128]{1,0:T(8,128)(2,1)} %param.12), channel_id=1, source_target_pairs={{0,16},{1,17},{2,18},{3,19},{4,20},{5,21},{6,22},{7,23},{8,24},{9,... | collective-permute-start | bytes 98312 | tf_op jit(solution)/shard_map/ppermute | solution.py:397
  6.3 10.9 %collective-permute-start.5 = (bf16[128,128]{1,0:T(8,128)(2,1)}, bf16[128,128]{1,0:T(8,128)(2,1)S(1)}, u32[]{:S(2)}, u32[]{:S(2)}) collective-permute-start(bf16[128,128]{1,0:T(8,128)(2,1)} %param.12), channel_id=1, source_target_pairs={{0,24},{1,25},{2,26},{3,27},{4,28},{5,29},{6,30},{7,31},{8,16},{9,... | collective-permute-start | bytes 98312 | tf_op jit(solution)/shard_map/ppermute | solution.py:397
  8.7 20.2 %all-to-all-start = ((bf16[32,8,256]{2,1,0:T(8,128)(2,1)}), bf16[32,8,256]{2,1,0:T(8,128)(2,1)S(1)}, u32[]{:S(2)}, u32[]{:S(2)}) async-start(bf16[32,8,256]{2,1,0:T(8,128)(2,1)} %bitcast.4), calls=%async_computation | async-start | bytes 262144 | tf_op jit(solution)/shard_map/all_to_all | solution.py:422
  16.1 16.9 %collective-permute-start.1 = (bf16[2560,128]{1,0:T(8,128)(2,1)S(1)}, bf16[2560,128]{1,0:T(8,128)(2,1)S(1)}, u32[]{:S(2)}, u32[]{:S(2)}) collective-permute-start(bf16[2560,128]{1,0:T(8,128)(2,1)S(1)} %slice.53), channel_id=1, source_target_pairs={{0,1},{1,0},{2,3},{3,2},{4,5},{5,4},{6,7},{7,6},{8,9},{9,8},{10,11... | collective-permute-start | bytes 1966088 | tf_op jit(solution)/shard_map/ppermute | solution.py:397
  17.3 4.8 %collective-permute-start.6 = (bf16[4,64,128]{2,1,0:T(8,128)(2,1)S(1)}, bf16[4,64,128]{2,1,0:T(8,128)(2,1)S(1)}, u32[]{:S(2)}, u32[]{:S(2)}) collective-permute-start(bf16[4,64,128]{2,1,0:T(8,128)(2,1)S(1)} %get-tuple-element.53), channel_id=1, source_target_pairs={{0,2},{1,3},{2,0},{3,1},{4,6},{5,7},{6,4},{7,5},{8,10},{9,11},{10,... | collective-permute-start | bytes 196616 | tf_op jit(solution)/shard_map/ppermute | solution.py:397
  19.0 4.9 %collective-permute-start.8 = (bf16[4,64,128]{2,1,0:T(8,128)(2,1)S(1)}, bf16[4,64,128]{2,1,0:T(8,128)(2,1)S(1)}, u32[]{:S(2)}, u32[]{:S(2)}) collective-permute-start(bf16[4,64,128]{2,1,0:T(8,128)(2,1)S(1)} %get-tuple-element.51), channel_id=1, source_target_pairs={{0,4},{1,5},{2,6},{3,7},{4,0},{5,1},{6,2},{7,3},{8,12},{9,13},{10,... | collective-permute-start | bytes 196616 | tf_op jit(solution)/shard_map/ppermute | solution.py:397
  22.1 5.1 %collective-permute-start.7 = (bf16[2,4,64,128]{3,2,1,0:T(8,128)(2,1)S(1)}, bf16[2,4,64,128]{3,2,1,0:T(8,128)(2,1)S(1)}, u32[]{:S(2)}, u32[]{:S(2)}) collective-permute-start(bf16[2,4,64,128]{3,2,1,0:T(8,128)(2,1)S(1)} %pad_maximum_fusion.even_refs_0_), channel_id=1, source_target_pairs={{0,4},{1,5},{2,6},{3,7},{4,0},{5,1},{6,2},{7,3},{8,12},{9,13},{10,... | collective-permute-start | bytes 393224 | tf_op jit(solution)/shard_map/ppermute | solution.py:397
  23.9 5.0 %collective-permute-start.9 = (bf16[2,4,64,128]{3,2,1,0:T(8,128)(2,1)S(1)}, bf16[2,4,64,128]{3,2,1,0:T(8,128)(2,1)S(1)}, u32[]{:S(2)}, u32[]{:S(2)}) collective-permute-start(bf16[2,4,64,128]{3,2,1,0:T(8,128)(2,1)S(1)} %pad_maximum_fusion.1.even_refs_2_), channel_id=1, source_target_pairs={{0,2},{1,3},{2,0},{3,1},{4,6},{5,7},{6,4},{7,5},{8,10},{9,11},{10,... | collective-permute-start | bytes 393224 | tf_op jit(solution)/shard_map/ppermute | solution.py:397
  25.1 6.5 %collective-permute-start.10 = (bf16[2,4,64,128]{3,2,1,0:T(8,128)(2,1)S(1)}, bf16[2,4,64,128]{3,2,1,0:T(8,128)(2,1)S(1)}, u32[]{:S(2)}, u32[]{:S(2)}) collective-permute-start(bf16[2,4,64,128]{3,2,1,0:T(8,128)(2,1)S(1)} %pad_maximum_fusion.even_refs_0_), channel_id=1, source_target_pairs={{0,1},{1,0},{2,3},{3,2},{4,5},{5,4},{6,7},{7,6},{8,9},{9,8},{10,11... | collective-permute-start | bytes 393224 | tf_op jit(solution)/shard_map/ppermute | solution.py:397
  25.1 1.6 %collective-permute-start = (s32[1]{0:T(128)}, s32[1]{0:T(128)}, u32[]{:S(2)}, u32[]{:S(2)}) collective-permute-start(s32[1]{0:T(128)} %param.17), channel_id=1, source_target_pairs={{0,1},{1,0},{2,3},{3,2},{4,5},{5,4},{6,7},{7,6},{8,9},{9,8},{10,11... | collective-permute-start | bytes 20 | tf_op jit(solution)/shard_map/ppermute | solution.py:397
  26.7 6.1 %collective-permute-start.12 = (bf16[2,4,64,128]{3,2,1,0:T(8,128)(2,1)S(1)}, bf16[2,4,64,128]{3,2,1,0:T(8,128)(2,1)S(1)}, u32[]{:S(2)}, u32[]{:S(2)}) collective-permute-start(bf16[2,4,64,128]{3,2,1,0:T(8,128)(2,1)S(1)} %pad_maximum_fusion.1.even_refs_2_), channel_id=1, source_target_pairs={{0,1},{1,0},{2,3},{3,2},{4,5},{5,4},{6,7},{7,6},{8,9},{9,8},{10,11... | collective-permute-start | bytes 393224 | tf_op jit(solution)/shard_map/ppermute | solution.py:397
  27.2 5.9 %collective-permute-start.11 = (bf16[2,4,64,128]{3,2,1,0:T(8,128)(2,1)S(1)}, bf16[2,4,64,128]{3,2,1,0:T(8,128)(2,1)S(1)}, u32[]{:S(2)}, u32[]{:S(2)}) collective-permute-start(bf16[2,4,64,128]{3,2,1,0:T(8,128)(2,1)S(1)} %collective-permute-done.7.even_refs_1_), channel_id=1, source_target_pairs={{0,1},{1,0},{2,3},{3,2},{4,5},{5,4},{6,7},{7,6},{8,9},{9,8},{10,11... | collective-permute-start | bytes 393224 | tf_op jit(solution)/shard_map/ppermute | solution.py:397
  28.9 4.1 %collective-permute-start.13 = (bf16[2,4,64,128]{3,2,1,0:T(8,128)(2,1)S(1)}, bf16[2,4,64,128]{3,2,1,0:T(8,128)(2,1)S(1)}, u32[]{:S(2)}, u32[]{:S(2)}) collective-permute-start(bf16[2,4,64,128]{3,2,1,0:T(8,128)(2,1)S(1)} %collective-permute-done.9.even_refs_3_), channel_id=1, source_target_pairs={{0,1},{1,0},{2,3},{3,2},{4,5},{5,4},{6,7},{7,6},{8,9},{9,8},{10,11... | collective-permute-start | bytes 393224 | tf_op jit(solution)/shard_map/ppermute | solution.py:397
  28.9 4.2 %copy-start = (f32[5120,128]{1,0:T(8,128)S(1)}, f32[5120,128]{1,0:T(8,128)}, u32[]{:S(2)}) copy-start(f32[5120,128]{1,0:T(8,128)} %state_ref.3) | copy-start | bytes 7864324
  28.9 4.2 %copy-start.1 = (f32[2,1024]{1,0:T(2,128)S(1)}, f32[2,1024]{1,0:T(2,128)}, u32[]{:S(2)}) copy-start(f32[2,1024]{1,0:T(2,128)} %gains_ref.1) | copy-start | bytes 24580
  28.9 4.2 %copy-start.2 = (f32[128]{0:T(128)S(1)}, f32[128]{0:T(128)}, u32[]{:S(2)}) copy-start(f32[128]{0:T(128)} %param.14) | copy-start | bytes 1540
  31.6 1.4 %collective-permute-start.2 = (f32[2,24,256]{2,1,0:T(8,128)S(1)}, f32[2,24,256]{2,1,0:T(8,128)S(1)}, u32[]{:S(2)}, u32[]{:S(2)}) collective-permute-start(f32[2,24,256]{2,1,0:T(8,128)S(1)} %get-tuple-element.28), channel_id=1, source_target_pairs={{0,1},{1,0},{2,3},{3,2},{4,5},{5,4},{6,7},{7,6},{8,9},{9,8},{10,11... | collective-permute-start | bytes 147464 | tf_op jit(solution)/shard_map/ppermute | solution.py:397
  65.7 2.0 %collective-permute-start.15 = (bf16[2,2,2,4,64,128]{5,4,3,2,1,0:T(8,128)(2,1)S(1)}, bf16[2,2,2,4,64,128]{5,4,3,2,1,0:T(8,128)(2,1)S(1)}, u32[]{:S(2)}, u32[]{:S(2)}) collective-permute-start(bf16[2,2,2,4,64,128]{5,4,3,2,1,0:T(8,128)(2,1)S(1)} %bitcast.36), channel_id=1, source_target_pairs={{0,1},{1,0},{2,3},{3,2},{4,5},{5,4},{6,7},{7,6},{8,9},{9,8},{10,11... | collective-permute-start | bytes 1572872 | tf_op jit(solution)/shard_map/ppermute | solution.py:397
  66.0 17.3 %collective-permute-start.14 = (bf16[2816,128]{1,0:T(8,128)(2,1)S(1)}, bf16[2816,128]{1,0:T(8,128)(2,1)S(1)}, u32[]{:S(2)}, u32[]{:S(2)}) collective-permute-start(bf16[2816,128]{1,0:T(8,128)(2,1)S(1)} %get-tuple-element.34), channel_id=1, source_target_pairs={{0,1},{1,0},{2,3},{3,2},{4,5},{5,4},{6,7},{7,6},{8,9},{9,8},{10,11... | collective-permute-start | bytes 2162696 | tf_op jit(solution)/shard_map/ppermute | solution.py:397
  67.8 5.7 %collective-permute-start.16 = (bf16[2,4,64,128]{3,2,1,0:T(8,128)(2,1)S(1)}, bf16[2,4,64,128]{3,2,1,0:T(8,128)(2,1)S(1)}, u32[]{:S(2)}, u32[]{:S(2)}) collective-permute-start(bf16[2,4,64,128]{3,2,1,0:T(8,128)(2,1)S(1)} %get-tuple-element.38), channel_id=1, source_target_pairs={{0,2},{1,3},{2,0},{3,1},{4,6},{5,7},{6,4},{7,5},{8,10},{9,11},{10,... | collective-permute-start | bytes 393224 | tf_op jit(solution)/shard_map/ppermute | solution.py:397
  67.9 5.7 %collective-permute-start.17 = (bf16[2,4,64,128]{3,2,1,0:T(8,128)(2,1)S(1)}, bf16[2,4,64,128]{3,2,1,0:T(8,128)(2,1)S(1)}, u32[]{:S(2)}, u32[]{:S(2)}) collective-permute-start(bf16[2,4,64,128]{3,2,1,0:T(8,128)(2,1)S(1)} %get-tuple-element.40), channel_id=1, source_target_pairs={{0,4},{1,5},{2,6},{3,7},{4,0},{5,1},{6,2},{7,3},{8,12},{9,13},{10,... | collective-permute-start | bytes 393224 | tf_op jit(solution)/shard_map/ppermute | solution.py:397
  73.6 4.3 %collective-permute-start.18 = (bf16[4,64,128]{2,1,0:T(8,128)(2,1)S(1)}, bf16[4,64,128]{2,1,0:T(8,128)(2,1)S(1)}, u32[]{:S(2)}, u32[]{:S(2)}) collective-permute-start(bf16[4,64,128]{2,1,0:T(8,128)(2,1)S(1)} %get-tuple-element.42), channel_id=1, source_target_pairs={{0,4},{1,5},{2,6},{3,7},{4,0},{5,1},{6,2},{7,3},{8,12},{9,13},{10,... | collective-permute-start | bytes 196616 | tf_op jit(solution)/shard_map/ppermute | solution.py:397
  74.6 4.3 %collective-permute-start.19 = (bf16[4,64,128]{2,1,0:T(8,128)(2,1)S(1)}, bf16[4,64,128]{2,1,0:T(8,128)(2,1)S(1)}, u32[]{:S(2)}, u32[]{:S(2)}) collective-permute-start(bf16[4,64,128]{2,1,0:T(8,128)(2,1)S(1)} %get-tuple-element.44), channel_id=1, source_target_pairs={{0,2},{1,3},{2,0},{3,1},{4,6},{5,7},{6,4},{7,5},{8,10},{9,11},{10,... | collective-permute-start | bytes 196616 | tf_op jit(solution)/shard_map/ppermute | solution.py:397
  78.9 7.4 %collective-permute-start.20 = (bf16[128,128]{1,0:T(8,128)(2,1)S(1)}, bf16[128,128]{1,0:T(8,128)(2,1)S(1)}, u32[]{:S(2)}, u32[]{:S(2)}) collective-permute-start(bf16[128,128]{1,0:T(8,128)(2,1)S(1)} %get-tuple-element.46), channel_id=1, source_target_pairs={{0,8},{1,9},{2,10},{3,11},{4,12},{5,13},{6,14},{7,15},{8,0},{9,1},... | collective-permute-start | bytes 98312 | tf_op jit(solution)/shard_map/ppermute | solution.py:397
  80.4 5.9 %collective-permute-start.21 = (bf16[128,128]{1,0:T(8,128)(2,1)S(1)}, bf16[128,128]{1,0:T(8,128)(2,1)S(1)}, u32[]{:S(2)}, u32[]{:S(2)}) collective-permute-start(bf16[128,128]{1,0:T(8,128)(2,1)S(1)} %get-tuple-element.47), channel_id=1, source_target_pairs={{0,16},{1,17},{2,18},{3,19},{4,20},{5,21},{6,22},{7,23},{8,24},{9,... | collective-permute-start | bytes 98312 | tf_op jit(solution)/shard_map/ppermute | solution.py:397
  80.4 5.9 %collective-permute-start.22 = (bf16[128,128]{1,0:T(8,128)(2,1)S(1)}, bf16[128,128]{1,0:T(8,128)(2,1)S(1)}, u32[]{:S(2)}, u32[]{:S(2)}) collective-permute-start(bf16[128,128]{1,0:T(8,128)(2,1)S(1)} %get-tuple-element.48), channel_id=1, source_target_pairs={{0,24},{1,25},{2,26},{3,27},{4,28},{5,29},{6,30},{7,31},{8,16},{9,... | collective-permute-start | bytes 98312 | tf_op jit(solution)/shard_map/ppermute | solution.py:397

commit v2 on v1

--- a/solution.py
+++ b/solution.py
@@ -46,14 +46,24 @@
     tgt_hbm,
     tile_hbm,
     gap_hbm,
+    forcing_hbm,
     out_ref,
     count_ref,
+    first_ref,
+    second_ref,
     tgt_ref,
     tile_ref,
     gap_ref,
     sems,
 ):
-    pairs = ((tgt_hbm, tgt_ref), (tile_hbm, tile_ref), (gap_hbm, gap_ref))
+    half = first_ref.shape[0]
+    pairs = (
+        (tgt_hbm, tgt_ref),
+        (tile_hbm, tile_ref),
+        (gap_hbm, gap_ref),
+        (forcing_hbm.at[pl.ds(0, half)], first_ref),
+        (forcing_hbm.at[pl.ds(half, half)], second_ref),
+    )
     copies = [pltpu.make_async_copy(*pair, sems.at[place]) for place, pair in enumerate(pairs)]
     for copy in copies:
         copy.start()
@@ -181,6 +191,7 @@
     index_ref,
     scalar_ref,
     out_ref,
+    h_ref,
     sem,
     out_sems,
 ):
@@ -192,7 +203,7 @@
     all_tiles = own_tiles + taken
     lines = mine_ref.shape[1]
     last_line = 2 * lines
-    guest_rows = guest_ref.shape[0]
+    guest_rows = guest_tend_ref.shape[0] - ROWS
     lanes = index_ref.shape[1]
     parts = ROWS // lanes
     part_lines = last_line + 8
@@ -260,7 +271,7 @@
 
         @pl.when(jnp.logical_not(is_own))
         def _():
-            x_ref[chain] = guest_ref[pl.ds(start, ROWS), :]
+            x_ref[chain] = guest_ref[pl.ds(start, ROWS), :].astype(BF16)
             gap_ref[chain] = jnp.broadcast_to(guest_mine_ref[1, pl.ds(index, 1), :], (8, ROWS))
 
     def store(chain, step, tend):
@@ -290,24 +301,31 @@
             out_ref.at[chain], tend_ref.at[pl.ds(0, ROWS)], out_sems.at[chain]
         ).wait()
 
-    def two_tiles(step, _):
-        chains = range(2)
+    chains = range(2)
+
+    def load_pair(step):
         for chain in chains:
             load(chain, 2 * step + chain)
-        inputs = []
-        for chain in chains:
-            gap = jnp.transpose(gap_ref[chain])[:, 0:1]
-            forcing = rows_ref[chain * ROWS : (chain + 1) * ROWS, :] + gap * lapse_ref[...]
-            inputs.append(jnp.concatenate([forcing.astype(BF16), x_ref[chain]], axis=1))
-        fetch(step + 1)
+
+    def enter(chain):
+        gap = jnp.transpose(gap_ref[chain])[:, 0:1]
+        forcing = rows_ref[chain * ROWS : (chain + 1) * ROWS, :] + gap * lapse_ref[...]
+        inputs = jnp.concatenate([forcing.astype(BF16), x_ref[chain]], axis=1)
+        h_ref[chain] = jnp.dot(inputs, w_in_ref[...], preferred_element_type=F32)
+
+    def two_tiles(step, _):
+        load_pair(step + 1)
         spread(step - 1)
-        h = [jnp.dot(v, w_in_ref[...], preferred_element_type=F32) for v in inputs]
-        low = [norm(v, gains_ref[0:1, :]) for v in h]
+        low = [norm(h_ref[chain], gains_ref[0:1, :]) for chain in chains]
         up = [jnp.dot(v, w_up_ref[...], preferred_element_type=F32) for v in low]
         active = [(v * (0.5 + 0.5 * jnp.tanh(0.5 * v))).astype(BF16) for v in up]
         h = [
-            v + jnp.dot(a, w_down_ref[...], preferred_element_type=F32) for v, a in zip(h, active)
+            h_ref[chain] + jnp.dot(active[chain], w_down_ref[...], preferred_element_type=F32)
+            for chain in chains
         ]
+        for chain in chains:
+            enter(chain)
+        fetch(step + 2)
         low = [norm(v, gains_ref[1:2, :]) for v in h]
         result = [jnp.dot(v, w_out_ref[...], preferred_element_type=F32) for v in low]
         for chain in chains:
@@ -320,6 +338,10 @@
 
     steps = (all_tiles + 1) // 2
     fetch(0)
+    load_pair(0)
+    for chain in chains:
+        enter(chain)
+    fetch(1)
     lax.fori_loop(0, steps, two_tiles, 0)
     spread(steps - 1)
     chunk = min(half, 128)
@@ -397,19 +419,22 @@
         return lax.ppermute(values, AXES, [(i, i ^ bit) for i in range(devices)])
 
     small = pltpu.CompilerParams(vmem_limit_bytes=24 << 20)
-    buckets, counts = pl.pallas_call(
+    half = tiles // 2
+    buckets, counts, own_first, own_second = pl.pallas_call(
         functools.partial(bucket_kernel, devices, capacity),
         out_shape=(
             jax.ShapeDtypeStruct((devices * FIELDS, places), BF16),
             jax.ShapeDtypeStruct((tiles, width), F32),
+            jax.ShapeDtypeStruct((half, width), BF16),
+            jax.ShapeDtypeStruct((half, width), BF16),
         ),
-        in_specs=[HBM] * 3,
-        out_specs=(VMEM,) * 2,
+        in_specs=[HBM] * 4,
+        out_specs=(VMEM,) * 4,
         scratch_shapes=[
             pltpu.VMEM((1, columns), jnp.int32),
             pltpu.VMEM((1, columns), jnp.int32),
             pltpu.VMEM((1, columns), F32),
-            pltpu.SemaphoreType.DMA((3,)),
+            pltpu.SemaphoreType.DMA((5,)),
         ],
         cost_estimate=cost(3.0),
         compiler_params=small,
@@ -418,15 +443,17 @@
         hbm(column_target.reshape(1, columns)),
         hbm(column_tile.reshape(1, columns)),
         hbm(elevation_gap.reshape(1, columns)),
+        hbm(tile_forcing),
     )
     got = lax.all_to_all(
         buckets.reshape(devices, FIELDS, places), AXES, split_axis=0, concat_axis=0, tiled=True
     )
     far = 1 << (bits - 3)
-    half = tiles // 2
-    gathered = [tile_forcing] + [swap(tile_forcing, s << 3) for s in range(1, far)]
-    first = jnp.stack([piece[:half] for piece in gathered])
-    second = jnp.stack([piece[half:] for piece in gathered])
+    gathered = []
+    for s in range(1, far):
+        gathered.append(swap(tile_forcing, s << 3))
+    first = jnp.stack([own_first] + [piece[:half] for piece in gathered])
+    second = jnp.stack([own_second] + [piece[half:] for piece in gathered])
     first = jnp.stack([first, swap(first, 2)])
     second = jnp.stack([second, swap(second, 4)])
     even = (first, swap(first, 4), second, swap(second, 2))
@@ -434,7 +461,7 @@
     odd = tuple(swap(piece, 1) for piece in even)
 
     other_count = swap(owner_counts, 1)
-    guest_state = swap(land_state[:guest_rows].astype(BF16), 1)
+    guest_state = swap(land_state, 1)
 
     weights = (w_in, w_up[0], w_down[0], w_out)
     mine, theirs, weights = pl.pallas_call(
@@ -456,8 +483,8 @@
     table_rows = devices * tiles
     held = vmem if table_rows <= 8192 else hbm
     network_bytes = (
-        (12 << 20)
-        + (capacity + guest_rows) * width * 8
+        (14 << 20)
+        + capacity * width * 12
         + table_rows * width * (4 * (5 if table_rows <= 8192 else 2) + 10)
     )
     if table_rows > 8192:
@@ -482,6 +509,7 @@
             pltpu.VMEM((ROWS // width * (2 * meta_rows + 8), width), jnp.int32),
             pltpu.SMEM((ROWS // width * (2 * meta_rows + 8), width), jnp.int32),
             pltpu.VMEM((2, ROWS, width), BF16),
+            pltpu.VMEM((2, ROWS, w_in.shape[1]), F32),
             pltpu.SemaphoreType.DMA,
             pltpu.SemaphoreType.DMA((2,)),
         ],
@@ -492,7 +520,7 @@
         owner_counts,
         other_count,
         land_state,
-        guest_state,
+        held(guest_state),
         mine,
         guest_mine,
         tuple(held(piece) for piece in even),
@@ -537,7 +565,10 @@
         second,
         swap(second_out, 2),
     )
-    parts = [swap(part, s << 3) for s, part in zip(range(1, far), parts)]
+    here = []
+    for s, part in zip(range(1, far), parts):
+        here.append(swap(part, s << 3))
+    parts = here
     for part in parts:
         sums = sums + part.astype(F32)
     tile_flux = sums / jnp.maximum(counts, 1.0)

time: 87.5 us -> 84.7 us (0.968)
  local copies, waits for them, and re-layouts: 2.15 us -> 0.66 us
    slice x1 -> x0, local copies, waits for them, and re-layouts: 1.38 us -> none  [local(): guest_state = swap(land_state[:guest_rows].astype(BF16), 1)]
    all_to_all x1, starting transfers between devices: 6.07 us -> 5.17 us  [local(): lax.all_to_all(buckets.reshape(devices, FIELDS, places), AXES, split_axis...]
  transfers between devices with their start and end apart: 24 -> 24, of which waited for: 10 -> 10; matrix products, arithmetic and copies ran while one was open for 3% -> 0% of each run, Pallas kernels for 9% -> 10%
where the time goes in v2:
time: 84.7 us; the launch traced here: 84.4 us
  Pallas kernels  40.2 us (47%)
  starting transfers between devices  28.4 us (34%)
  waiting for transfers between devices  12.8 us (15%)
  between operations  1.5 us (2%)
    pallas_call x1, Pallas kernels, local(): pl.pallas_call(network_kernel, out_shape=(jax.ShapeDtypeStruct((capacity,...  32 us
    ppermute x23, starting transfers between devices, swap(): return lax.ppermute(values, AXES, [(i, i ^ bit) for i in range(devices)])  23.3 us
    ppermute x23, waiting for transfers between devices, swap(): return lax.ppermute(values, AXES, [(i, i ^ bit) for i in range(devices)])  12.8 us
    all_to_all x1, starting transfers between devices, local(): lax.all_to_all(buckets.reshape(devices, FIELDS, places), AXES, split_axis...  5.17 us
    pallas_call x1, Pallas kernels, local(): pl.pallas_call(finish_kernel, out_shape=jax.ShapeDtypeStruct((capacity, w...  3.02 us
    pallas_call x1, Pallas kernels, local(): pl.pallas_call(functools.partial(arrange_kernel, devices, tiles), out_sha...  2.65 us
    pallas_call x1, Pallas kernels, local(): pl.pallas_call(functools.partial(bucket_kernel, devices, capacity), out_s...  2.41 us
  transfers between devices with their start and end apart: 24, of which 10 were waited for; matrix products, arithmetic and copies ran while one was open for 0% of the time, Pallas kernels for 10%

profile of v2, /device:TPU:0, one launch (start us, length us, event | category | flops | bytes accessed | tf_op | source)
XLA Modules:
  0.0 84.4 jit_solution(9854105043679767388)
XLA Ops:
  0.6 0.6 collective-permute-start.1
  1.2 2.6 %collective-permute-start.3 = (bf16[128,128]{1,0:T(8,128)(2,1)}, bf16[128,128]{1,0:T(8,128)(2,1)S(1)}, u32[]{:S(2)}, u32[]{:S(2)}) collective-permute-start(bf16[128,128]{1,0:T(8,128)(2,1)} %forcing_hbm.1), channel_id=1, source_target_pairs={{0,8},{1,9},{2,10},{3,11},{4,12},{5,13},{6,14},{7,15},{8,0},{9,1},... | collective-permute-start | bytes 98312 | tf_op jit(solution)/shard_map/ppermute | solution.py:419
  3.8 2.5 %collective-permute-start.5 = (bf16[128,128]{1,0:T(8,128)(2,1)}, bf16[128,128]{1,0:T(8,128)(2,1)S(1)}, u32[]{:S(2)}, u32[]{:S(2)}) collective-permute-start(bf16[128,128]{1,0:T(8,128)(2,1)} %forcing_hbm.1), channel_id=1, source_target_pairs={{0,24},{1,25},{2,26},{3,27},{4,28},{5,29},{6,30},{7,31},{8,16},{9,... | collective-permute-start | bytes 98312 | tf_op jit(solution)/shard_map/ppermute | solution.py:419
  6.3 0.1 collective-permute-start.4
  6.4 2.4 %bucket.1 = (bf16[256,256]{1,0:T(8,128)(2,1)}, f32[128,128]{1,0:T(8,128)S(1)}, bf16[64,128]{1,0:T(8,128)(2,1)S(1)}, bf16[64,128]{1,0:T(8,128)(2,1)S(1)}) custom-call(s32[1,2048]{1,0:T(1,128)} %bitcast.41, s32[1,2048]{1,0:T(1,128)} %bitcast.42, f32[1,2048]{1,0:T(1,128)} %bitcast.43, bf16[128,128]{1,0:T(8,128)(2,1)} %forcing_hbm.1), custom_call_target="tpu_custom_call" | custom-call | flops 24000000 | bytes 6000000 | tf_op jit(solution)/shard_map/bucket/pallas_call | solution.py:423
  8.8 0.0 copy-start.1
  8.8 0.6 copy-done.1
  9.5 5.2 %all-to-all-start = ((bf16[32,8,256]{2,1,0:T(8,128)(2,1)}), bf16[32,8,256]{2,1,0:T(8,128)(2,1)S(1)}, u32[]{:S(2)}, u32[]{:S(2)}) async-start(bf16[32,8,256]{2,1,0:T(8,128)(2,1)} %bitcast.4), calls=%async_computation | async-start | bytes 262144 | tf_op jit(solution)/shard_map/all_to_all | solution.py:448
  14.6 0.0 collective-permute-done.3
  14.7 0.0 collective-permute-done.5
  14.7 0.0 collective-permute-done.4
  14.7 1.8 %collective-permute-start.8 = (bf16[4,64,128]{2,1,0:T(8,128)(2,1)S(1)}, bf16[4,64,128]{2,1,0:T(8,128)(2,1)S(1)}, u32[]{:S(2)}, u32[]{:S(2)}) collective-permute-start(bf16[4,64,128]{2,1,0:T(8,128)(2,1)S(1)} %get-tuple-element.55), channel_id=1, source_target_pairs={{0,4},{1,5},{2,6},{3,7},{4,0},{5,1},{6,2},{7,3},{8,12},{9,13},{10,... | collective-permute-start | bytes 196616 | tf_op jit(solution)/shard_map/ppermute | solution.py:419
  16.6 1.5 %collective-permute-start.6 = (bf16[4,64,128]{2,1,0:T(8,128)(2,1)S(1)}, bf16[4,64,128]{2,1,0:T(8,128)(2,1)S(1)}, u32[]{:S(2)}, u32[]{:S(2)}) collective-permute-start(bf16[4,64,128]{2,1,0:T(8,128)(2,1)S(1)} %get-tuple-element.57), channel_id=1, source_target_pairs={{0,2},{1,3},{2,0},{3,1},{4,6},{5,7},{6,4},{7,5},{8,10},{9,11},{10,... | collective-permute-start | bytes 196616 | tf_op jit(solution)/shard_map/ppermute | solution.py:419
  18.1 1.5 %collective-permute-done.8 = bf16[4,64,128]{2,1,0:T(8,128)(2,1)S(1)} collective-permute-done((bf16[4,64,128]{2,1,0:T(8,128)(2,1)S(1)}, bf16[4,64,128]{2,1,0:T(8,128)(2,1)S(1)}, u32[]{:S(2)}, u32[]{:S(2)}) %collective-permute-start.8) | collective-permute-done | bytes 65568 | tf_op jit(solution)/shard_map/ppermute | solution.py:419
  19.7 1.8 %collective-permute-start.9 = (bf16[2,4,64,128]{3,2,1,0:T(8,128)(2,1)S(1)}, bf16[2,4,64,128]{3,2,1,0:T(8,128)(2,1)S(1)}, u32[]{:S(2)}, u32[]{:S(2)}) collective-permute-start(bf16[2,4,64,128]{3,2,1,0:T(8,128)(2,1)S(1)} %pad_maximum_fusion.1.even_refs_2_), channel_id=1, source_target_pairs={{0,2},{1,3},{2,0},{3,1},{4,6},{5,7},{6,4},{7,5},{8,10},{9,11},{10,... | collective-permute-start | bytes 393224 | tf_op jit(solution)/shard_map/ppermute | solution.py:419
  21.5 0.0 collective-permute-done.6
  21.5 1.4 %collective-permute-start.7 = (bf16[2,4,64,128]{3,2,1,0:T(8,128)(2,1)S(1)}, bf16[2,4,64,128]{3,2,1,0:T(8,128)(2,1)S(1)}, u32[]{:S(2)}, u32[]{:S(2)}) collective-permute-start(bf16[2,4,64,128]{3,2,1,0:T(8,128)(2,1)S(1)} %pad_maximum_fusion.even_refs_0_), channel_id=1, source_target_pairs={{0,4},{1,5},{2,6},{3,7},{4,0},{5,1},{6,2},{7,3},{8,12},{9,13},{10,... | collective-permute-start | bytes 393224 | tf_op jit(solution)/shard_map/ppermute | solution.py:419
  22.8 0.0 collective-permute-start.12
  22.8 0.5 collective-permute-start
  23.4 1.0 %collective-permute-done.other_ref = s32[1]{0:T(128)} collective-permute-done((s32[1]{0:T(128)}, s32[1]{0:T(128)}, u32[]{:S(2)}, u32[]{:S(2)}) %collective-permute-start) | collective-permute-done | bytes 36 | tf_op jit(solution)/shard_map/ppermute | solution.py:419
  24.3 0.3 collective-permute-start.10
  24.6 0.1 collective-permute-done.9.even_refs_3_
  24.7 0.1 collective-permute-start.13
  24.8 1.7 %collective-permute-done.7.even_refs_1_ = bf16[2,4,64,128]{3,2,1,0:T(8,128)(2,1)S(1)} collective-permute-done((bf16[2,4,64,128]{3,2,1,0:T(8,128)(2,1)S(1)}, bf16[2,4,64,128]{3,2,1,0:T(8,128)(2,1)S(1)}, u32[]{:S(2)}, u32[]{:S(2)}) %collective-permute-start.7) | collective-permute-done | bytes 131104 | tf_op jit(solution)/shard_map/ppermute | solution.py:419
  26.5 0.0 collective-permute-start.11
  26.5 0.0 all-to-all-done
  26.5 0.0 copy-start
  26.5 0.0 copy-start.3
  26.5 0.0 copy-start.4
  26.6 2.7 %arrange.1 = (f32[2,24,256]{2,1,0:T(8,128)S(1)}, f32[2,24,256]{2,1,0:T(8,128)S(1)}, bf16[256,1024]{1,0:T(8,128)(2,1)S(1)}, bf16[1024,1024]{1,0:T(8,128)(2,1)S(1)...) custom-call(s32[1]{0:T(128)} %bitcast.me_ref, bf16[256,256]{1,0:T(8,128)(2,1)S(1)} %bitcast.32, ...), custom_call_target="tpu_custom_call" | custom-call | flops 32000000 | bytes 8000000 | tf_op jit(solution)/shard_map/arrange/pallas_call | solution.py:467
  29.2 0.0 collective-permute-done.12.odd_refs_2_
  29.2 0.6 collective-permute-start.2
  30.4 0.0 collective-permute-done.10.odd_refs_0_
  30.4 0.2 collective-permute-done.2.guest_mine_ref
  30.7 0.0 collective-permute-done.13.odd_refs_3_
  30.7 0.0 collective-permute-done.11.odd_refs_1_
  30.7 0.0 collective-permute-done.1.guest_ref
  30.7 0.0 copy-done
  30.7 0.0 copy-done.3
  30.7 0.0 copy-done.4
  30.7 32.0 %network.1 = (bf16[5120,128]{1,0:T(8,128)(2,1)S(1)}, bf16[2816,128]{1,0:T(8,128)(2,1)S(1)}, f32[2048,128]{1,0:T(8,128)S(1)}, bf16[2048,128]{1,0:T(8,128)(2,1)S(1)}) custom-call(s32[1]{0:T(128)S(6)} %copy.14.own_ref, s32[1]{0:T(128)} %collective-permute-done.other_ref, f32[5120,128]{1,0:T(8,128)S(1)} %copy-done, ...), custom_call_target="tpu_custom_call" | custom-call | flops 400000000 | bytes 100000000 | tf_op jit(solution)/shard_map/network/pallas_call | solution.py:492
  62.7 0.2 collective-permute-start.15
  62.9 0.3 collective-permute-start.14
  63.3 1.4 %collective-permute-done.15.in_ref = bf16[2,2,2,4,64,128]{5,4,3,2,1,0:T(8,128)(2,1)S(1)} collective-permute-done((bf16[2,2,2,4,64,128]{5,4,3,2,1,0:T(8,128)(2,1)S(1)}, bf16[2,2,2,4,64,128]{5,4,3,2,1,0:T(8,128)(2,1)S(1)}, u32[]{:S(2)}, u32[]{:S(2)}) %collective-permute-start.15) | collective-permute-done | bytes 524320 | tf_op jit(solution)/shard_map/ppermute | solution.py:419
  64.7 0.1 add.22
  64.8 0.1 collective-permute-start.16
  64.8 1.3 %collective-permute-start.17 = (bf16[2,4,64,128]{3,2,1,0:T(8,128)(2,1)S(1)}, bf16[2,4,64,128]{3,2,1,0:T(8,128)(2,1)S(1)}, u32[]{:S(2)}, u32[]{:S(2)}) collective-permute-start(bf16[2,4,64,128]{3,2,1,0:T(8,128)(2,1)S(1)} %get-tuple-element.44), channel_id=1, source_target_pairs={{0,4},{1,5},{2,6},{3,7},{4,0},{5,1},{6,2},{7,3},{8,12},{9,13},{10,... | collective-permute-start | bytes 393224 | tf_op jit(solution)/shard_map/ppermute | solution.py:419
  66.2 4.2 %collective-permute-done.16.a_in_ref = bf16[2,4,64,128]{3,2,1,0:T(8,128)(2,1)S(1)} collective-permute-done((bf16[2,4,64,128]{3,2,1,0:T(8,128)(2,1)S(1)}, bf16[2,4,64,128]{3,2,1,0:T(8,128)(2,1)S(1)}, u32[]{:S(2)}, u32[]{:S(2)}) %collective-permute-start.16) | collective-permute-done | bytes 131104 | tf_op jit(solution)/shard_map/ppermute | solution.py:419
  70.4 0.1 collective-permute-done.17.b_in_ref
  70.5 1.4 %collective-permute-start.18 = (bf16[4,64,128]{2,1,0:T(8,128)(2,1)S(1)}, bf16[4,64,128]{2,1,0:T(8,128)(2,1)S(1)}, u32[]{:S(2)}, u32[]{:S(2)}) collective-permute-start(bf16[4,64,128]{2,1,0:T(8,128)(2,1)S(1)} %get-tuple-element.46), channel_id=1, source_target_pairs={{0,4},{1,5},{2,6},{3,7},{4,0},{5,1},{6,2},{7,3},{8,12},{9,13},{10,... | collective-permute-start | bytes 196616 | tf_op jit(solution)/shard_map/ppermute | solution.py:419
  71.9 1.7 %collective-permute-start.19 = (bf16[4,64,128]{2,1,0:T(8,128)(2,1)S(1)}, bf16[4,64,128]{2,1,0:T(8,128)(2,1)S(1)}, u32[]{:S(2)}, u32[]{:S(2)}) collective-permute-start(bf16[4,64,128]{2,1,0:T(8,128)(2,1)S(1)} %get-tuple-element.48), channel_id=1, source_target_pairs={{0,2},{1,3},{2,0},{3,1},{4,6},{5,7},{6,4},{7,5},{8,10},{9,11},{10,... | collective-permute-start | bytes 196616 | tf_op jit(solution)/shard_map/ppermute | solution.py:419
  73.6 1.3 %collective-permute-done.18.a_in_ref = bf16[4,64,128]{2,1,0:T(8,128)(2,1)S(1)} collective-permute-done((bf16[4,64,128]{2,1,0:T(8,128)(2,1)S(1)}, bf16[4,64,128]{2,1,0:T(8,128)(2,1)S(1)}, u32[]{:S(2)}, u32[]{:S(2)}) %collective-permute-start.18) | collective-permute-done | bytes 65568 | tf_op jit(solution)/shard_map/ppermute | solution.py:419
  74.9 1.3 %collective-permute-done.19.b_in_ref = bf16[4,64,128]{2,1,0:T(8,128)(2,1)S(1)} collective-permute-done((bf16[4,64,128]{2,1,0:T(8,128)(2,1)S(1)}, bf16[4,64,128]{2,1,0:T(8,128)(2,1)S(1)}, u32[]{:S(2)}, u32[]{:S(2)}) %collective-permute-start.19) | collective-permute-done | bytes 65568 | tf_op jit(solution)/shard_map/ppermute | solution.py:419
  76.2 1.6 %collective-permute-start.20 = (bf16[128,128]{1,0:T(8,128)(2,1)S(1)}, bf16[128,128]{1,0:T(8,128)(2,1)S(1)}, u32[]{:S(2)}, u32[]{:S(2)}) collective-permute-start(bf16[128,128]{1,0:T(8,128)(2,1)S(1)} %get-tuple-element.50), channel_id=1, source_target_pairs={{0,8},{1,9},{2,10},{3,11},{4,12},{5,13},{6,14},{7,15},{8,0},{9,1},... | collective-permute-start | bytes 98312 | tf_op jit(solution)/shard_map/ppermute | solution.py:419
  77.8 0.0 collective-permute-start.21
  77.8 2.8 %collective-permute-start.22 = (bf16[128,128]{1,0:T(8,128)(2,1)S(1)}, bf16[128,128]{1,0:T(8,128)(2,1)S(1)}, u32[]{:S(2)}, u32[]{:S(2)}) collective-permute-start(bf16[128,128]{1,0:T(8,128)(2,1)S(1)} %get-tuple-element.52), channel_id=1, source_target_pairs={{0,24},{1,25},{2,26},{3,27},{4,28},{5,29},{6,30},{7,31},{8,16},{9,... | collective-permute-start | bytes 98312 | tf_op jit(solution)/shard_map/ppermute | solution.py:419
  80.6 0.0 collective-permute-done.14.back_ref
  80.6 0.0 copy-start.2
  80.6 3.0 %finish.1 = f32[5120,128]{1,0:T(8,128)} custom-call(s32[1]{0:T(128)S(6)} %copy.14.own_ref, s32[1]{0:T(128)} %collective-permute-done.other_ref, f32[5120,128]{1,0:T(8,128)S(1)} %copy-done, bf16[5120,128]{1,0:T(8,128)(2,1)S(1)} %get-tuple-element.37.tend_ref, bf16[2816,128]{1,0:T(8,128)(2,1)S(1)} %collective-permute-done.14.back_ref), custom_call_target="tpu_custom_call" | custom-call | flops 32000000 | bytes 8000000 | tf_op jit(solution)/shard_map/finish/pallas_call | solution.py:578
  83.7 0.0 collective-permute-done.20
  83.7 0.0 collective-permute-done.21
  83.7 0.0 collective-permute-done.22
  83.7 0.0 copy-done.2
  83.7 0.7 maximum_divide_fusion
  (9 shorter events, 0.1 us)
Async XLA Ops:
  0.6 30.0 %collective-permute-start.1 = (f32[5120,128]{1,0:T(8,128)}, f32[5120,128]{1,0:T(8,128)S(1)}, u32[]{:S(2)}, u32[]{:S(2)}) collective-permute-start(f32[5120,128]{1,0:T(8,128)} %state_ref.3), channel_id=1, source_target_pairs={{0,1},{1,0},{2,3},{3,2},{4,5},{5,4},{6,7},{7,6},{8,9},{9,8},{10,11... | collective-permute-start | bytes 7864328 | tf_op jit(solution)/shard_map/ppermute | solution.py:419
  1.2 13.5 %collective-permute-start.3 = (bf16[128,128]{1,0:T(8,128)(2,1)}, bf16[128,128]{1,0:T(8,128)(2,1)S(1)}, u32[]{:S(2)}, u32[]{:S(2)}) collective-permute-start(bf16[128,128]{1,0:T(8,128)(2,1)} %forcing_hbm.1), channel_id=1, source_target_pairs={{0,8},{1,9},{2,10},{3,11},{4,12},{5,13},{6,14},{7,15},{8,0},{9,1},... | collective-permute-start | bytes 98312 | tf_op jit(solution)/shard_map/ppermute | solution.py:419
  3.8 10.8 %collective-permute-start.5 = (bf16[128,128]{1,0:T(8,128)(2,1)}, bf16[128,128]{1,0:T(8,128)(2,1)S(1)}, u32[]{:S(2)}, u32[]{:S(2)}) collective-permute-start(bf16[128,128]{1,0:T(8,128)(2,1)} %forcing_hbm.1), channel_id=1, source_target_pairs={{0,24},{1,25},{2,26},{3,27},{4,28},{5,29},{6,30},{7,31},{8,16},{9,... | collective-permute-start | bytes 98312 | tf_op jit(solution)/shard_map/ppermute | solution.py:419
  6.3 8.4 %collective-permute-start.4 = (bf16[128,128]{1,0:T(8,128)(2,1)}, bf16[128,128]{1,0:T(8,128)(2,1)S(1)}, u32[]{:S(2)}, u32[]{:S(2)}) collective-permute-start(bf16[128,128]{1,0:T(8,128)(2,1)} %forcing_hbm.1), channel_id=1, source_target_pairs={{0,16},{1,17},{2,18},{3,19},{4,20},{5,21},{6,22},{7,23},{8,24},{9,... | collective-permute-start | bytes 98312 | tf_op jit(solution)/shard_map/ppermute | solution.py:419
  8.8 0.6 copy-start.1
  9.5 17.1 %all-to-all-start = ((bf16[32,8,256]{2,1,0:T(8,128)(2,1)}), bf16[32,8,256]{2,1,0:T(8,128)(2,1)S(1)}, u32[]{:S(2)}, u32[]{:S(2)}) async-start(bf16[32,8,256]{2,1,0:T(8,128)(2,1)} %bitcast.4), calls=%async_computation | async-start | bytes 262144 | tf_op jit(solution)/shard_map/all_to_all | solution.py:448
  14.7 4.9 %collective-permute-start.8 = (bf16[4,64,128]{2,1,0:T(8,128)(2,1)S(1)}, bf16[4,64,128]{2,1,0:T(8,128)(2,1)S(1)}, u32[]{:S(2)}, u32[]{:S(2)}) collective-permute-start(bf16[4,64,128]{2,1,0:T(8,128)(2,1)S(1)} %get-tuple-element.55), channel_id=1, source_target_pairs={{0,4},{1,5},{2,6},{3,7},{4,0},{5,1},{6,2},{7,3},{8,12},{9,13},{10,... | collective-permute-start | bytes 196616 | tf_op jit(solution)/shard_map/ppermute | solution.py:419
  16.6 4.9 %collective-permute-start.6 = (bf16[4,64,128]{2,1,0:T(8,128)(2,1)S(1)}, bf16[4,64,128]{2,1,0:T(8,128)(2,1)S(1)}, u32[]{:S(2)}, u32[]{:S(2)}) collective-permute-start(bf16[4,64,128]{2,1,0:T(8,128)(2,1)S(1)} %get-tuple-element.57), channel_id=1, source_target_pairs={{0,2},{1,3},{2,0},{3,1},{4,6},{5,7},{6,4},{7,5},{8,10},{9,11},{10,... | collective-permute-start | bytes 196616 | tf_op jit(solution)/shard_map/ppermute | solution.py:419
  19.7 5.0 %collective-permute-start.9 = (bf16[2,4,64,128]{3,2,1,0:T(8,128)(2,1)S(1)}, bf16[2,4,64,128]{3,2,1,0:T(8,128)(2,1)S(1)}, u32[]{:S(2)}, u32[]{:S(2)}) collective-permute-start(bf16[2,4,64,128]{3,2,1,0:T(8,128)(2,1)S(1)} %pad_maximum_fusion.1.even_refs_2_), channel_id=1, source_target_pairs={{0,2},{1,3},{2,0},{3,1},{4,6},{5,7},{6,4},{7,5},{8,10},{9,11},{10,... | collective-permute-start | bytes 393224 | tf_op jit(solution)/shard_map/ppermute | solution.py:419
  21.5 5.0 %collective-permute-start.7 = (bf16[2,4,64,128]{3,2,1,0:T(8,128)(2,1)S(1)}, bf16[2,4,64,128]{3,2,1,0:T(8,128)(2,1)S(1)}, u32[]{:S(2)}, u32[]{:S(2)}) collective-permute-start(bf16[2,4,64,128]{3,2,1,0:T(8,128)(2,1)S(1)} %pad_maximum_fusion.even_refs_0_), channel_id=1, source_target_pairs={{0,4},{1,5},{2,6},{3,7},{4,0},{5,1},{6,2},{7,3},{8,12},{9,13},{10,... | collective-permute-start | bytes 393224 | tf_op jit(solution)/shard_map/ppermute | solution.py:419
  22.8 6.4 %collective-permute-start.12 = (bf16[2,4,64,128]{3,2,1,0:T(8,128)(2,1)S(1)}, bf16[2,4,64,128]{3,2,1,0:T(8,128)(2,1)S(1)}, u32[]{:S(2)}, u32[]{:S(2)}) collective-permute-start(bf16[2,4,64,128]{3,2,1,0:T(8,128)(2,1)S(1)} %pad_maximum_fusion.1.even_refs_2_), channel_id=1, source_target_pairs={{0,1},{1,0},{2,3},{3,2},{4,5},{5,4},{6,7},{7,6},{8,9},{9,8},{10,11... | collective-permute-start | bytes 393224 | tf_op jit(solution)/shard_map/ppermute | solution.py:419
  22.8 1.5 %collective-permute-start = (s32[1]{0:T(128)}, s32[1]{0:T(128)}, u32[]{:S(2)}, u32[]{:S(2)}) collective-permute-start(s32[1]{0:T(128)} %param.17), channel_id=1, source_target_pairs={{0,1},{1,0},{2,3},{3,2},{4,5},{5,4},{6,7},{7,6},{8,9},{9,8},{10,11... | collective-permute-start | bytes 20 | tf_op jit(solution)/shard_map/ppermute | solution.py:419
  24.3 6.1 %collective-permute-start.10 = (bf16[2,4,64,128]{3,2,1,0:T(8,128)(2,1)S(1)}, bf16[2,4,64,128]{3,2,1,0:T(8,128)(2,1)S(1)}, u32[]{:S(2)}, u32[]{:S(2)}) collective-permute-start(bf16[2,4,64,128]{3,2,1,0:T(8,128)(2,1)S(1)} %pad_maximum_fusion.even_refs_0_), channel_id=1, source_target_pairs={{0,1},{1,0},{2,3},{3,2},{4,5},{5,4},{6,7},{7,6},{8,9},{9,8},{10,11... | collective-permute-start | bytes 393224 | tf_op jit(solution)/shard_map/ppermute | solution.py:419
  24.7 6.0 %collective-permute-start.13 = (bf16[2,4,64,128]{3,2,1,0:T(8,128)(2,1)S(1)}, bf16[2,4,64,128]{3,2,1,0:T(8,128)(2,1)}, u32[]{:S(2)}, u32[]{:S(2)}) collective-permute-start(bf16[2,4,64,128]{3,2,1,0:T(8,128)(2,1)S(1)} %collective-permute-done.9.even_refs_3_), channel_id=1, source_target_pairs={{0,1},{1,0},{2,3},{3,2},{4,5},{5,4},{6,7},{7,6},{8,9},{9,8},{10,11... | collective-permute-start | bytes 393224 | tf_op jit(solution)/shard_map/ppermute | solution.py:419
  26.5 4.1 %collective-permute-start.11 = (bf16[2,4,64,128]{3,2,1,0:T(8,128)(2,1)S(1)}, bf16[2,4,64,128]{3,2,1,0:T(8,128)(2,1)}, u32[]{:S(2)}, u32[]{:S(2)}) collective-permute-start(bf16[2,4,64,128]{3,2,1,0:T(8,128)(2,1)S(1)} %collective-permute-done.7.even_refs_1_), channel_id=1, source_target_pairs={{0,1},{1,0},{2,3},{3,2},{4,5},{5,4},{6,7},{7,6},{8,9},{9,8},{10,11... | collective-permute-start | bytes 393224 | tf_op jit(solution)/shard_map/ppermute | solution.py:419
  26.5 4.2 %copy-start = (f32[5120,128]{1,0:T(8,128)S(1)}, f32[5120,128]{1,0:T(8,128)}, u32[]{:S(2)}) copy-start(f32[5120,128]{1,0:T(8,128)} %state_ref.3) | copy-start | bytes 7864324
  26.5 4.2 %copy-start.3 = (f32[2,1024]{1,0:T(2,128)S(1)}, f32[2,1024]{1,0:T(2,128)}, u32[]{:S(2)}) copy-start(f32[2,1024]{1,0:T(2,128)} %gains_ref.1) | copy-start | bytes 24580
  26.5 4.2 %copy-start.4 = (f32[128]{0:T(128)S(1)}, f32[128]{0:T(128)}, u32[]{:S(2)}) copy-start(f32[128]{0:T(128)} %param.14) | copy-start | bytes 1540
  29.2 1.4 %collective-permute-start.2 = (f32[2,24,256]{2,1,0:T(8,128)S(1)}, f32[2,24,256]{2,1,0:T(8,128)S(1)}, u32[]{:S(2)}, u32[]{:S(2)}) collective-permute-start(f32[2,24,256]{2,1,0:T(8,128)S(1)} %get-tuple-element.30), channel_id=1, source_target_pairs={{0,1},{1,0},{2,3},{3,2},{4,5},{5,4},{6,7},{7,6},{8,9},{9,8},{10,11... | collective-permute-start | bytes 147464 | tf_op jit(solution)/shard_map/ppermute | solution.py:419
  62.7 2.0 %collective-permute-start.15 = (bf16[2,2,2,4,64,128]{5,4,3,2,1,0:T(8,128)(2,1)S(1)}, bf16[2,2,2,4,64,128]{5,4,3,2,1,0:T(8,128)(2,1)S(1)}, u32[]{:S(2)}, u32[]{:S(2)}) collective-permute-start(bf16[2,2,2,4,64,128]{5,4,3,2,1,0:T(8,128)(2,1)S(1)} %bitcast.36), channel_id=1, source_target_pairs={{0,1},{1,0},{2,3},{3,2},{4,5},{5,4},{6,7},{7,6},{8,9},{9,8},{10,11... | collective-permute-start | bytes 1572872 | tf_op jit(solution)/shard_map/ppermute | solution.py:419
  62.9 17.7 %collective-permute-start.14 = (bf16[2816,128]{1,0:T(8,128)(2,1)S(1)}, bf16[2816,128]{1,0:T(8,128)(2,1)S(1)}, u32[]{:S(2)}, u32[]{:S(2)}) collective-permute-start(bf16[2816,128]{1,0:T(8,128)(2,1)S(1)} %get-tuple-element.38), channel_id=1, source_target_pairs={{0,1},{1,0},{2,3},{3,2},{4,5},{5,4},{6,7},{7,6},{8,9},{9,8},{10,11... | collective-permute-start | bytes 2162696 | tf_op jit(solution)/shard_map/ppermute | solution.py:419
  64.8 5.6 %collective-permute-start.16 = (bf16[2,4,64,128]{3,2,1,0:T(8,128)(2,1)S(1)}, bf16[2,4,64,128]{3,2,1,0:T(8,128)(2,1)S(1)}, u32[]{:S(2)}, u32[]{:S(2)}) collective-permute-start(bf16[2,4,64,128]{3,2,1,0:T(8,128)(2,1)S(1)} %get-tuple-element.42), channel_id=1, source_target_pairs={{0,2},{1,3},{2,0},{3,1},{4,6},{5,7},{6,4},{7,5},{8,10},{9,11},{10,... | collective-permute-start | bytes 393224 | tf_op jit(solution)/shard_map/ppermute | solution.py:419
  64.8 5.6 %collective-permute-start.17 = (bf16[2,4,64,128]{3,2,1,0:T(8,128)(2,1)S(1)}, bf16[2,4,64,128]{3,2,1,0:T(8,128)(2,1)S(1)}, u32[]{:S(2)}, u32[]{:S(2)}) collective-permute-start(bf16[2,4,64,128]{3,2,1,0:T(8,128)(2,1)S(1)} %get-tuple-element.44), channel_id=1, source_target_pairs={{0,4},{1,5},{2,6},{3,7},{4,0},{5,1},{6,2},{7,3},{8,12},{9,13},{10,... | collective-permute-start | bytes 393224 | tf_op jit(solution)/shard_map/ppermute | solution.py:419
  70.5 4.3 %collective-permute-start.18 = (bf16[4,64,128]{2,1,0:T(8,128)(2,1)S(1)}, bf16[4,64,128]{2,1,0:T(8,128)(2,1)S(1)}, u32[]{:S(2)}, u32[]{:S(2)}) collective-permute-start(bf16[4,64,128]{2,1,0:T(8,128)(2,1)S(1)} %get-tuple-element.46), channel_id=1, source_target_pairs={{0,4},{1,5},{2,6},{3,7},{4,0},{5,1},{6,2},{7,3},{8,12},{9,13},{10,... | collective-permute-start | bytes 196616 | tf_op jit(solution)/shard_map/ppermute | solution.py:419
  71.9 4.3 %collective-permute-start.19 = (bf16[4,64,128]{2,1,0:T(8,128)(2,1)S(1)}, bf16[4,64,128]{2,1,0:T(8,128)(2,1)S(1)}, u32[]{:S(2)}, u32[]{:S(2)}) collective-permute-start(bf16[4,64,128]{2,1,0:T(8,128)(2,1)S(1)} %get-tuple-element.48), channel_id=1, source_target_pairs={{0,2},{1,3},{2,0},{3,1},{4,6},{5,7},{6,4},{7,5},{8,10},{9,11},{10,... | collective-permute-start | bytes 196616 | tf_op jit(solution)/shard_map/ppermute | solution.py:419
  76.2 7.5 %collective-permute-start.20 = (bf16[128,128]{1,0:T(8,128)(2,1)S(1)}, bf16[128,128]{1,0:T(8,128)(2,1)S(1)}, u32[]{:S(2)}, u32[]{:S(2)}) collective-permute-start(bf16[128,128]{1,0:T(8,128)(2,1)S(1)} %get-tuple-element.50), channel_id=1, source_target_pairs={{0,8},{1,9},{2,10},{3,11},{4,12},{5,13},{6,14},{7,15},{8,0},{9,1},... | collective-permute-start | bytes 98312 | tf_op jit(solution)/shard_map/ppermute | solution.py:419
  77.8 5.9 %collective-permute-start.21 = (bf16[128,128]{1,0:T(8,128)(2,1)S(1)}, bf16[128,128]{1,0:T(8,128)(2,1)S(1)}, u32[]{:S(2)}, u32[]{:S(2)}) collective-permute-start(bf16[128,128]{1,0:T(8,128)(2,1)S(1)} %get-tuple-element.51), channel_id=1, source_target_pairs={{0,16},{1,17},{2,18},{3,19},{4,20},{5,21},{6,22},{7,23},{8,24},{9,... | collective-permute-start | bytes 98312 | tf_op jit(solution)/shard_map/ppermute | solution.py:419
  77.8 5.9 %collective-permute-start.22 = (bf16[128,128]{1,0:T(8,128)(2,1)S(1)}, bf16[128,128]{1,0:T(8,128)(2,1)S(1)}, u32[]{:S(2)}, u32[]{:S(2)}) collective-permute-start(bf16[128,128]{1,0:T(8,128)(2,1)S(1)} %get-tuple-element.52), channel_id=1, source_target_pairs={{0,24},{1,25},{2,26},{3,27},{4,28},{5,29},{6,30},{7,31},{8,16},{9,... | collective-permute-start | bytes 98312 | tf_op jit(solution)/shard_map/ppermute | solution.py:419
  80.6 3.0 %copy-start.2 = (f32[128,128]{1,0:T(8,128)S(1)}, f32[128,128]{1,0:T(8,128)}, u32[]{:S(2)}) copy-start(f32[128,128]{1,0:T(8,128)} %copy-done.1) | copy-start | bytes 196612

commit v3 on v2

--- a/solution.py
+++ b/solution.py
@@ -48,7 +48,6 @@
     gap_hbm,
     forcing_hbm,
     out_ref,
-    count_ref,
     first_ref,
     second_ref,
     tgt_ref,
@@ -71,7 +70,6 @@
         copy.wait()
     columns = tgt_ref.shape[1]
     places = out_ref.shape[1]
-    tiles = count_ref.shape[0]
     target = tgt_ref[...]
     peer = jnp.floor((target.astype(F32) + 0.5) * (1.0 / capacity)).astype(jnp.int32)
     slot = target - peer * capacity
@@ -114,10 +112,6 @@
         [jnp.where(peer == device, fields, 0.0) for device in range(devices)], axis=0
     ).astype(BF16)
     out_ref[...] = dot_nt(spread, place_hot).astype(BF16)
-    tile_hot = jnp.where(iota((tiles, columns), 0) == tile, 1.0, 0.0).astype(BF16)
-    count_ref[...] = jnp.dot(
-        tile_hot, jnp.ones((columns, count_ref.shape[1]), BF16), preferred_element_type=F32
-    )
 
 
 def arrange_kernel(devices, tiles, me_ref, got_ref, weight_hbms, mine_ref, guest_ref, weight_refs, sems):
@@ -359,7 +353,14 @@
         arrived(chain)
 
 
-def finish_kernel(own_ref, other_ref, state_ref, tend_ref, back_ref, out_ref):
+def finish_kernel(own_ref, other_ref, state_ref, tend_ref, back_ref, tile_ref, out_ref, count_ref):
+    @pl.when(pl.program_id(0) == 0)
+    def _():
+        tiles, columns = count_ref.shape[0], tile_ref.shape[1]
+        hot = jnp.where(iota((tiles, columns), 0) == tile_ref[...], 1.0, 0.0).astype(BF16)
+        ones = jnp.ones((columns, count_ref.shape[1]), BF16)
+        count_ref[...] = jnp.dot(hot, ones, preferred_element_type=F32)
+
     own = own_ref[0]
     given, _ = tile_ranges(own, other_ref[0])
     rows = out_ref.shape[0]
@@ -420,16 +421,15 @@
 
     small = pltpu.CompilerParams(vmem_limit_bytes=24 << 20)
     half = tiles // 2
-    buckets, counts, own_first, own_second = pl.pallas_call(
+    buckets, own_first, own_second = pl.pallas_call(
         functools.partial(bucket_kernel, devices, capacity),
         out_shape=(
             jax.ShapeDtypeStruct((devices * FIELDS, places), BF16),
-            jax.ShapeDtypeStruct((tiles, width), F32),
             jax.ShapeDtypeStruct((half, width), BF16),
             jax.ShapeDtypeStruct((half, width), BF16),
         ),
         in_specs=[HBM] * 4,
-        out_specs=(VMEM,) * 4,
+        out_specs=(VMEM,) * 3,
         scratch_shapes=[
             pltpu.VMEM((1, columns), jnp.int32),
             pltpu.VMEM((1, columns), jnp.int32),
@@ -571,21 +571,28 @@
     parts = here
     for part in parts:
         sums = sums + part.astype(F32)
-    tile_flux = sums / jnp.maximum(counts, 1.0)
-
     part = guest_rows // 2
     wide = pl.BlockSpec((part, width), lambda i: (i, 0))
-    new_state = pl.pallas_call(
+    new_state, counts = pl.pallas_call(
         finish_kernel,
-        out_shape=jax.ShapeDtypeStruct((capacity, width), F32),
+        out_shape=(
+            jax.ShapeDtypeStruct((capacity, width), F32),
+            jax.ShapeDtypeStruct((tiles, width), F32),
+        ),
         grid=(-(-capacity // part),),
         in_specs=[SMEM] * 2
-        + [wide, wide, pl.BlockSpec((part, width), lambda i: (jnp.minimum(i, 1), 0))],
-        out_specs=wide,
+        + [
+            wide,
+            wide,
+            pl.BlockSpec((part, width), lambda i: (jnp.minimum(i, 1), 0)),
+            pl.BlockSpec((1, columns), lambda i: (0, 0)),
+        ],
+        out_specs=(wide, pl.BlockSpec((tiles, width), lambda i: (0, 0))),
         cost_estimate=cost(4.0),
         compiler_params=small,
         name="finish",
-    )(owner_counts, other_count, land_state, tend, back)
+    )(owner_counts, other_count, land_state, tend, back, column_tile.reshape(1, columns))
+    tile_flux = sums / jnp.maximum(counts, 1.0)
     return (new_state, tile_flux)
 
 

time: 84.7 us -> 84.4 us (level)
  no operation moved by 1% of the time
where the time goes in v3:
time: 84.4 us; the launch traced here: 84 us
  Pallas kernels  40.5 us (48%)
  starting transfers between devices  28.4 us (34%)
  waiting for transfers between devices  12.8 us (15%)
  between operations  1.49 us (2%)
    pallas_call x1, Pallas kernels, local(): pl.pallas_call(network_kernel, out_shape=(jax.ShapeDtypeStruct((capacity,...  32 us
    ppermute x23, starting transfers between devices, swap(): return lax.ppermute(values, AXES, [(i, i ^ bit) for i in range(devices)])  23.3 us
    ppermute x23, waiting for transfers between devices, swap(): return lax.ppermute(values, AXES, [(i, i ^ bit) for i in range(devices)])  12.8 us
    all_to_all x1, starting transfers between devices, local(): lax.all_to_all(buckets.reshape(devices, FIELDS, places), AXES, split_axis...  5.18 us
    pallas_call x1, Pallas kernels, local(): pl.pallas_call(finish_kernel, out_shape=(jax.ShapeDtypeStruct((capacity,...  3.28 us
    pallas_call x1, Pallas kernels, local(): pl.pallas_call(functools.partial(arrange_kernel, devices, tiles), out_sha...  2.65 us
    pallas_call x1, Pallas kernels, local(): pl.pallas_call(functools.partial(bucket_kernel, devices, capacity), out_s...  2.39 us
  transfers between devices with their start and end apart: 24, of which 10 were waited for; matrix products, arithmetic and copies ran while one was open for 0% of the time, Pallas kernels for 10%

profile of v3, /device:TPU:0, one launch (start us, length us, event | category | flops | bytes accessed | tf_op | source)
XLA Modules:
  0.0 84.0 jit_solution(522711903687459541)
XLA Ops:
  0.6 0.6 collective-permute-start.1
  1.2 2.6 %collective-permute-start.3 = (bf16[128,128]{1,0:T(8,128)(2,1)}, bf16[128,128]{1,0:T(8,128)(2,1)S(1)}, u32[]{:S(2)}, u32[]{:S(2)}) collective-permute-start(bf16[128,128]{1,0:T(8,128)(2,1)} %forcing_hbm.1), channel_id=1, source_target_pairs={{0,8},{1,9},{2,10},{3,11},{4,12},{5,13},{6,14},{7,15},{8,0},{9,1},... | collective-permute-start | bytes 98312 | tf_op jit(solution)/shard_map/ppermute | solution.py:420
  3.8 2.5 %collective-permute-start.5 = (bf16[128,128]{1,0:T(8,128)(2,1)}, bf16[128,128]{1,0:T(8,128)(2,1)S(1)}, u32[]{:S(2)}, u32[]{:S(2)}) collective-permute-start(bf16[128,128]{1,0:T(8,128)(2,1)} %forcing_hbm.1), channel_id=1, source_target_pairs={{0,24},{1,25},{2,26},{3,27},{4,28},{5,29},{6,30},{7,31},{8,16},{9,... | collective-permute-start | bytes 98312 | tf_op jit(solution)/shard_map/ppermute | solution.py:420
  6.3 0.1 collective-permute-start.4
  6.4 2.4 %bucket.1 = (bf16[256,256]{1,0:T(8,128)(2,1)}, bf16[64,128]{1,0:T(8,128)(2,1)S(1)}, bf16[64,128]{1,0:T(8,128)(2,1)S(1)}) custom-call(s32[1,2048]{1,0:T(1,128)} %bitcast.43, s32[1,2048]{1,0:T(1,128)} %bitcast.35, f32[1,2048]{1,0:T(1,128)} %bitcast.44, bf16[128,128]{1,0:T(8,128)(2,1)} %forcing_hbm.1), custom_call_target="tpu_custom_call" | custom-call | flops 24000000 | bytes 6000000 | tf_op jit(solution)/shard_map/bucket/pallas_call | solution.py:424
  8.8 5.2 %all-to-all-start = ((bf16[32,8,256]{2,1,0:T(8,128)(2,1)}), bf16[32,8,256]{2,1,0:T(8,128)(2,1)S(1)}, u32[]{:S(2)}, u32[]{:S(2)}) async-start(bf16[32,8,256]{2,1,0:T(8,128)(2,1)} %bitcast.4), calls=%async_computation | async-start | bytes 262144 | tf_op jit(solution)/shard_map/all_to_all | solution.py:448
  14.0 0.0 collective-permute-done.3
  14.0 0.0 collective-permute-done.5
  14.1 0.0 collective-permute-done.4
  14.1 1.8 %collective-permute-start.8 = (bf16[4,64,128]{2,1,0:T(8,128)(2,1)S(1)}, bf16[4,64,128]{2,1,0:T(8,128)(2,1)S(1)}, u32[]{:S(2)}, u32[]{:S(2)}) collective-permute-start(bf16[4,64,128]{2,1,0:T(8,128)(2,1)S(1)} %get-tuple-element.57), channel_id=1, source_target_pairs={{0,4},{1,5},{2,6},{3,7},{4,0},{5,1},{6,2},{7,3},{8,12},{9,13},{10,... | collective-permute-start | bytes 196616 | tf_op jit(solution)/shard_map/ppermute | solution.py:420
  15.9 1.5 %collective-permute-start.6 = (bf16[4,64,128]{2,1,0:T(8,128)(2,1)S(1)}, bf16[4,64,128]{2,1,0:T(8,128)(2,1)S(1)}, u32[]{:S(2)}, u32[]{:S(2)}) collective-permute-start(bf16[4,64,128]{2,1,0:T(8,128)(2,1)S(1)} %get-tuple-element.59), channel_id=1, source_target_pairs={{0,2},{1,3},{2,0},{3,1},{4,6},{5,7},{6,4},{7,5},{8,10},{9,11},{10,... | collective-permute-start | bytes 196616 | tf_op jit(solution)/shard_map/ppermute | solution.py:420
  17.5 1.5 %collective-permute-done.8 = bf16[4,64,128]{2,1,0:T(8,128)(2,1)S(1)} collective-permute-done((bf16[4,64,128]{2,1,0:T(8,128)(2,1)S(1)}, bf16[4,64,128]{2,1,0:T(8,128)(2,1)S(1)}, u32[]{:S(2)}, u32[]{:S(2)}) %collective-permute-start.8) | collective-permute-done | bytes 65568 | tf_op jit(solution)/shard_map/ppermute | solution.py:420
  19.0 1.8 %collective-permute-start.9 = (bf16[2,4,64,128]{3,2,1,0:T(8,128)(2,1)S(1)}, bf16[2,4,64,128]{3,2,1,0:T(8,128)(2,1)S(1)}, u32[]{:S(2)}, u32[]{:S(2)}) collective-permute-start(bf16[2,4,64,128]{3,2,1,0:T(8,128)(2,1)S(1)} %pad_maximum_fusion.1.even_refs_2_), channel_id=1, source_target_pairs={{0,2},{1,3},{2,0},{3,1},{4,6},{5,7},{6,4},{7,5},{8,10},{9,11},{10,... | collective-permute-start | bytes 393224 | tf_op jit(solution)/shard_map/ppermute | solution.py:420
  20.8 0.0 collective-permute-done.6
  20.9 1.4 %collective-permute-start.7 = (bf16[2,4,64,128]{3,2,1,0:T(8,128)(2,1)S(1)}, bf16[2,4,64,128]{3,2,1,0:T(8,128)(2,1)S(1)}, u32[]{:S(2)}, u32[]{:S(2)}) collective-permute-start(bf16[2,4,64,128]{3,2,1,0:T(8,128)(2,1)S(1)} %pad_maximum_fusion.even_refs_0_), channel_id=1, source_target_pairs={{0,4},{1,5},{2,6},{3,7},{4,0},{5,1},{6,2},{7,3},{8,12},{9,13},{10,... | collective-permute-start | bytes 393224 | tf_op jit(solution)/shard_map/ppermute | solution.py:420
  22.2 0.0 collective-permute-start.12
  22.2 0.5 collective-permute-start
  22.7 1.0 %collective-permute-done.other_ref = s32[1]{0:T(128)} collective-permute-done((s32[1]{0:T(128)}, s32[1]{0:T(128)}, u32[]{:S(2)}, u32[]{:S(2)}) %collective-permute-start) | collective-permute-done | bytes 36 | tf_op jit(solution)/shard_map/ppermute | solution.py:420
  23.7 0.3 collective-permute-start.10
  24.0 0.1 collective-permute-done.9.even_refs_3_
  24.1 0.1 collective-permute-start.13
  24.2 1.7 %collective-permute-done.7.even_refs_1_ = bf16[2,4,64,128]{3,2,1,0:T(8,128)(2,1)S(1)} collective-permute-done((bf16[2,4,64,128]{3,2,1,0:T(8,128)(2,1)S(1)}, bf16[2,4,64,128]{3,2,1,0:T(8,128)(2,1)S(1)}, u32[]{:S(2)}, u32[]{:S(2)}) %collective-permute-start.7) | collective-permute-done | bytes 131104 | tf_op jit(solution)/shard_map/ppermute | solution.py:420
  25.9 0.0 collective-permute-start.11
  25.9 0.0 all-to-all-done
  25.9 0.0 copy-start
  25.9 0.0 copy-start.2
  25.9 0.0 copy-start.3
  25.9 2.7 %arrange.1 = (f32[2,24,256]{2,1,0:T(8,128)S(1)}, f32[2,24,256]{2,1,0:T(8,128)S(1)}, bf16[256,1024]{1,0:T(8,128)(2,1)S(1)}, bf16[1024,1024]{1,0:T(8,128)(2,1)S(1)...) custom-call(s32[1]{0:T(128)} %bitcast.me_ref, bf16[256,256]{1,0:T(8,128)(2,1)S(1)} %bitcast.32, ...), custom_call_target="tpu_custom_call" | custom-call | flops 32000000 | bytes 8000000 | tf_op jit(solution)/shard_map/arrange/pallas_call | solution.py:467
  28.6 0.0 collective-permute-done.12.odd_refs_2_
  28.6 0.6 collective-permute-start.2
  29.8 0.0 collective-permute-done.10.odd_refs_0_
  29.8 0.2 collective-permute-done.2.guest_mine_ref
  30.0 0.0 collective-permute-done.13.odd_refs_3_
  30.0 0.0 collective-permute-done.11.odd_refs_1_
  30.0 0.0 collective-permute-done.1.guest_ref
  30.0 0.0 copy-done
  30.0 0.0 copy-done.2
  30.1 0.0 copy-done.3
  30.1 32.0 %network.1 = (bf16[5120,128]{1,0:T(8,128)(2,1)S(1)}, bf16[2816,128]{1,0:T(8,128)(2,1)S(1)}, f32[2048,128]{1,0:T(8,128)S(1)}, bf16[2048,128]{1,0:T(8,128)(2,1)S(1)}) custom-call(s32[1]{0:T(128)S(6)} %copy.14.own_ref, s32[1]{0:T(128)} %collective-permute-done.other_ref, f32[5120,128]{1,0:T(8,128)S(1)} %copy-done, ...), custom_call_target="tpu_custom_call" | custom-call | flops 400000000 | bytes 100000000 | tf_op jit(solution)/shard_map/network/pallas_call | solution.py:492
  62.1 0.0 copy-start.1
  62.1 0.2 collective-permute-start.15
  62.3 0.3 collective-permute-start.14
  62.7 1.4 %collective-permute-done.15.in_ref = bf16[2,2,2,4,64,128]{5,4,3,2,1,0:T(8,128)(2,1)S(1)} collective-permute-done((bf16[2,2,2,4,64,128]{5,4,3,2,1,0:T(8,128)(2,1)S(1)}, bf16[2,2,2,4,64,128]{5,4,3,2,1,0:T(8,128)(2,1)S(1)}, u32[]{:S(2)}, u32[]{:S(2)}) %collective-permute-start.15) | collective-permute-done | bytes 524320 | tf_op jit(solution)/shard_map/ppermute | solution.py:420
  64.1 0.1 add.22
  64.1 0.1 collective-permute-start.16
  64.2 1.3 %collective-permute-start.17 = (bf16[2,4,64,128]{3,2,1,0:T(8,128)(2,1)S(1)}, bf16[2,4,64,128]{3,2,1,0:T(8,128)(2,1)S(1)}, u32[]{:S(2)}, u32[]{:S(2)}) collective-permute-start(bf16[2,4,64,128]{3,2,1,0:T(8,128)(2,1)S(1)} %get-tuple-element.46), channel_id=1, source_target_pairs={{0,4},{1,5},{2,6},{3,7},{4,0},{5,1},{6,2},{7,3},{8,12},{9,13},{10,... | collective-permute-start | bytes 393224 | tf_op jit(solution)/shard_map/ppermute | solution.py:420
  65.6 4.2 %collective-permute-done.16.a_in_ref = bf16[2,4,64,128]{3,2,1,0:T(8,128)(2,1)S(1)} collective-permute-done((bf16[2,4,64,128]{3,2,1,0:T(8,128)(2,1)S(1)}, bf16[2,4,64,128]{3,2,1,0:T(8,128)(2,1)S(1)}, u32[]{:S(2)}, u32[]{:S(2)}) %collective-permute-start.16) | collective-permute-done | bytes 131104 | tf_op jit(solution)/shard_map/ppermute | solution.py:420
  69.8 0.1 collective-permute-done.17.b_in_ref
  69.9 1.4 %collective-permute-start.18 = (bf16[4,64,128]{2,1,0:T(8,128)(2,1)S(1)}, bf16[4,64,128]{2,1,0:T(8,128)(2,1)S(1)}, u32[]{:S(2)}, u32[]{:S(2)}) collective-permute-start(bf16[4,64,128]{2,1,0:T(8,128)(2,1)S(1)} %get-tuple-element.48), channel_id=1, source_target_pairs={{0,4},{1,5},{2,6},{3,7},{4,0},{5,1},{6,2},{7,3},{8,12},{9,13},{10,... | collective-permute-start | bytes 196616 | tf_op jit(solution)/shard_map/ppermute | solution.py:420
  71.3 1.7 %collective-permute-start.19 = (bf16[4,64,128]{2,1,0:T(8,128)(2,1)S(1)}, bf16[4,64,128]{2,1,0:T(8,128)(2,1)S(1)}, u32[]{:S(2)}, u32[]{:S(2)}) collective-permute-start(bf16[4,64,128]{2,1,0:T(8,128)(2,1)S(1)} %get-tuple-element.50), channel_id=1, source_target_pairs={{0,2},{1,3},{2,0},{3,1},{4,6},{5,7},{6,4},{7,5},{8,10},{9,11},{10,... | collective-permute-start | bytes 196616 | tf_op jit(solution)/shard_map/ppermute | solution.py:420
  72.9 1.3 %collective-permute-done.18.a_in_ref = bf16[4,64,128]{2,1,0:T(8,128)(2,1)S(1)} collective-permute-done((bf16[4,64,128]{2,1,0:T(8,128)(2,1)S(1)}, bf16[4,64,128]{2,1,0:T(8,128)(2,1)S(1)}, u32[]{:S(2)}, u32[]{:S(2)}) %collective-permute-start.18) | collective-permute-done | bytes 65568 | tf_op jit(solution)/shard_map/ppermute | solution.py:420
  74.2 1.3 %collective-permute-done.19.b_in_ref = bf16[4,64,128]{2,1,0:T(8,128)(2,1)S(1)} collective-permute-done((bf16[4,64,128]{2,1,0:T(8,128)(2,1)S(1)}, bf16[4,64,128]{2,1,0:T(8,128)(2,1)S(1)}, u32[]{:S(2)}, u32[]{:S(2)}) %collective-permute-start.19) | collective-permute-done | bytes 65568 | tf_op jit(solution)/shard_map/ppermute | solution.py:420
  75.6 1.6 %collective-permute-start.20 = (bf16[128,128]{1,0:T(8,128)(2,1)S(1)}, bf16[128,128]{1,0:T(8,128)(2,1)S(1)}, u32[]{:S(2)}, u32[]{:S(2)}) collective-permute-start(bf16[128,128]{1,0:T(8,128)(2,1)S(1)} %get-tuple-element.52), channel_id=1, source_target_pairs={{0,8},{1,9},{2,10},{3,11},{4,12},{5,13},{6,14},{7,15},{8,0},{9,1},... | collective-permute-start | bytes 98312 | tf_op jit(solution)/shard_map/ppermute | solution.py:420
  77.2 0.0 collective-permute-start.21
  77.2 2.8 %collective-permute-start.22 = (bf16[128,128]{1,0:T(8,128)(2,1)S(1)}, bf16[128,128]{1,0:T(8,128)(2,1)S(1)}, u32[]{:S(2)}, u32[]{:S(2)}) collective-permute-start(bf16[128,128]{1,0:T(8,128)(2,1)S(1)} %get-tuple-element.54), channel_id=1, source_target_pairs={{0,24},{1,25},{2,26},{3,27},{4,28},{5,29},{6,30},{7,31},{8,16},{9,... | collective-permute-start | bytes 98312 | tf_op jit(solution)/shard_map/ppermute | solution.py:420
  80.0 0.0 collective-permute-done.14.back_ref
  80.0 0.0 copy-done.1
  80.0 3.3 %finish.1 = (f32[5120,128]{1,0:T(8,128)}, f32[128,128]{1,0:T(8,128)S(1)}) custom-call(s32[1]{0:T(128)S(6)} %copy.14.own_ref, s32[1]{0:T(128)} %collective-permute-done.other_ref, f32[5120,128]{1,0:T(8,128)S(1)} %copy-done, bf16[5120,128]{1,0:T(8,128)(2,1)S(1)} %get-tuple-element.38.tend_ref, bf16[2816,128]{1,0:T(8,128)(2,1)S(1)} %collective-permute-done.14.back_ref, ...), custom_call_target="tpu_custom_call" | custom-call | flops 32000000 | bytes 8000000 | tf_op jit(solution)/shard_map/finish/pallas_call | solution.py:576
  83.3 0.0 collective-permute-done.20
  83.3 0.0 collective-permute-done.21
  83.3 0.0 collective-permute-done.22
  83.3 0.7 maximum_divide_fusion
  (9 shorter events, 0.1 us)
Async XLA Ops:
  0.6 29.4 %collective-permute-start.1 = (f32[5120,128]{1,0:T(8,128)}, f32[5120,128]{1,0:T(8,128)S(1)}, u32[]{:S(2)}, u32[]{:S(2)}) collective-permute-start(f32[5120,128]{1,0:T(8,128)} %state_ref.3), channel_id=1, source_target_pairs={{0,1},{1,0},{2,3},{3,2},{4,5},{5,4},{6,7},{7,6},{8,9},{9,8},{10,11... | collective-permute-start | bytes 7864328 | tf_op jit(solution)/shard_map/ppermute | solution.py:420
  1.2 12.8 %collective-permute-start.3 = (bf16[128,128]{1,0:T(8,128)(2,1)}, bf16[128,128]{1,0:T(8,128)(2,1)S(1)}, u32[]{:S(2)}, u32[]{:S(2)}) collective-permute-start(bf16[128,128]{1,0:T(8,128)(2,1)} %forcing_hbm.1), channel_id=1, source_target_pairs={{0,8},{1,9},{2,10},{3,11},{4,12},{5,13},{6,14},{7,15},{8,0},{9,1},... | collective-permute-start | bytes 98312 | tf_op jit(solution)/shard_map/ppermute | solution.py:420
  3.8 10.2 %collective-permute-start.5 = (bf16[128,128]{1,0:T(8,128)(2,1)}, bf16[128,128]{1,0:T(8,128)(2,1)S(1)}, u32[]{:S(2)}, u32[]{:S(2)}) collective-permute-start(bf16[128,128]{1,0:T(8,128)(2,1)} %forcing_hbm.1), channel_id=1, source_target_pairs={{0,24},{1,25},{2,26},{3,27},{4,28},{5,29},{6,30},{7,31},{8,16},{9,... | collective-permute-start | bytes 98312 | tf_op jit(solution)/shard_map/ppermute | solution.py:420
  6.3 7.7 %collective-permute-start.4 = (bf16[128,128]{1,0:T(8,128)(2,1)}, bf16[128,128]{1,0:T(8,128)(2,1)S(1)}, u32[]{:S(2)}, u32[]{:S(2)}) collective-permute-start(bf16[128,128]{1,0:T(8,128)(2,1)} %forcing_hbm.1), channel_id=1, source_target_pairs={{0,16},{1,17},{2,18},{3,19},{4,20},{5,21},{6,22},{7,23},{8,24},{9,... | collective-permute-start | bytes 98312 | tf_op jit(solution)/shard_map/ppermute | solution.py:420
  8.8 17.1 %all-to-all-start = ((bf16[32,8,256]{2,1,0:T(8,128)(2,1)}), bf16[32,8,256]{2,1,0:T(8,128)(2,1)S(1)}, u32[]{:S(2)}, u32[]{:S(2)}) async-start(bf16[32,8,256]{2,1,0:T(8,128)(2,1)} %bitcast.4), calls=%async_computation | async-start | bytes 262144 | tf_op jit(solution)/shard_map/all_to_all | solution.py:448
  14.1 4.9 %collective-permute-start.8 = (bf16[4,64,128]{2,1,0:T(8,128)(2,1)S(1)}, bf16[4,64,128]{2,1,0:T(8,128)(2,1)S(1)}, u32[]{:S(2)}, u32[]{:S(2)}) collective-permute-start(bf16[4,64,128]{2,1,0:T(8,128)(2,1)S(1)} %get-tuple-element.57), channel_id=1, source_target_pairs={{0,4},{1,5},{2,6},{3,7},{4,0},{5,1},{6,2},{7,3},{8,12},{9,13},{10,... | collective-permute-start | bytes 196616 | tf_op jit(solution)/shard_map/ppermute | solution.py:420
  15.9 4.9 %collective-permute-start.6 = (bf16[4,64,128]{2,1,0:T(8,128)(2,1)S(1)}, bf16[4,64,128]{2,1,0:T(8,128)(2,1)S(1)}, u32[]{:S(2)}, u32[]{:S(2)}) collective-permute-start(bf16[4,64,128]{2,1,0:T(8,128)(2,1)S(1)} %get-tuple-element.59), channel_id=1, source_target_pairs={{0,2},{1,3},{2,0},{3,1},{4,6},{5,7},{6,4},{7,5},{8,10},{9,11},{10,... | collective-permute-start | bytes 196616 | tf_op jit(solution)/shard_map/ppermute | solution.py:420
  19.0 5.0 %collective-permute-start.9 = (bf16[2,4,64,128]{3,2,1,0:T(8,128)(2,1)S(1)}, bf16[2,4,64,128]{3,2,1,0:T(8,128)(2,1)S(1)}, u32[]{:S(2)}, u32[]{:S(2)}) collective-permute-start(bf16[2,4,64,128]{3,2,1,0:T(8,128)(2,1)S(1)} %pad_maximum_fusion.1.even_refs_2_), channel_id=1, source_target_pairs={{0,2},{1,3},{2,0},{3,1},{4,6},{5,7},{6,4},{7,5},{8,10},{9,11},{10,... | collective-permute-start | bytes 393224 | tf_op jit(solution)/shard_map/ppermute | solution.py:420
  20.9 5.0 %collective-permute-start.7 = (bf16[2,4,64,128]{3,2,1,0:T(8,128)(2,1)S(1)}, bf16[2,4,64,128]{3,2,1,0:T(8,128)(2,1)S(1)}, u32[]{:S(2)}, u32[]{:S(2)}) collective-permute-start(bf16[2,4,64,128]{3,2,1,0:T(8,128)(2,1)S(1)} %pad_maximum_fusion.even_refs_0_), channel_id=1, source_target_pairs={{0,4},{1,5},{2,6},{3,7},{4,0},{5,1},{6,2},{7,3},{8,12},{9,13},{10,... | collective-permute-start | bytes 393224 | tf_op jit(solution)/shard_map/ppermute | solution.py:420
  22.2 6.4 %collective-permute-start.12 = (bf16[2,4,64,128]{3,2,1,0:T(8,128)(2,1)S(1)}, bf16[2,4,64,128]{3,2,1,0:T(8,128)(2,1)S(1)}, u32[]{:S(2)}, u32[]{:S(2)}) collective-permute-start(bf16[2,4,64,128]{3,2,1,0:T(8,128)(2,1)S(1)} %pad_maximum_fusion.1.even_refs_2_), channel_id=1, source_target_pairs={{0,1},{1,0},{2,3},{3,2},{4,5},{5,4},{6,7},{7,6},{8,9},{9,8},{10,11... | collective-permute-start | bytes 393224 | tf_op jit(solution)/shard_map/ppermute | solution.py:420
  22.2 1.5 %collective-permute-start = (s32[1]{0:T(128)}, s32[1]{0:T(128)}, u32[]{:S(2)}, u32[]{:S(2)}) collective-permute-start(s32[1]{0:T(128)} %param.17), channel_id=1, source_target_pairs={{0,1},{1,0},{2,3},{3,2},{4,5},{5,4},{6,7},{7,6},{8,9},{9,8},{10,11... | collective-permute-start | bytes 20 | tf_op jit(solution)/shard_map/ppermute | solution.py:420
  23.7 6.1 %collective-permute-start.10 = (bf16[2,4,64,128]{3,2,1,0:T(8,128)(2,1)S(1)}, bf16[2,4,64,128]{3,2,1,0:T(8,128)(2,1)S(1)}, u32[]{:S(2)}, u32[]{:S(2)}) collective-permute-start(bf16[2,4,64,128]{3,2,1,0:T(8,128)(2,1)S(1)} %pad_maximum_fusion.even_refs_0_), channel_id=1, source_target_pairs={{0,1},{1,0},{2,3},{3,2},{4,5},{5,4},{6,7},{7,6},{8,9},{9,8},{10,11... | collective-permute-start | bytes 393224 | tf_op jit(solution)/shard_map/ppermute | solution.py:420
  24.1 6.0 %collective-permute-start.13 = (bf16[2,4,64,128]{3,2,1,0:T(8,128)(2,1)S(1)}, bf16[2,4,64,128]{3,2,1,0:T(8,128)(2,1)}, u32[]{:S(2)}, u32[]{:S(2)}) collective-permute-start(bf16[2,4,64,128]{3,2,1,0:T(8,128)(2,1)S(1)} %collective-permute-done.9.even_refs_3_), channel_id=1, source_target_pairs={{0,1},{1,0},{2,3},{3,2},{4,5},{5,4},{6,7},{7,6},{8,9},{9,8},{10,11... | collective-permute-start | bytes 393224 | tf_op jit(solution)/shard_map/ppermute | solution.py:420
  25.9 4.1 %collective-permute-start.11 = (bf16[2,4,64,128]{3,2,1,0:T(8,128)(2,1)S(1)}, bf16[2,4,64,128]{3,2,1,0:T(8,128)(2,1)}, u32[]{:S(2)}, u32[]{:S(2)}) collective-permute-start(bf16[2,4,64,128]{3,2,1,0:T(8,128)(2,1)S(1)} %collective-permute-done.7.even_refs_1_), channel_id=1, source_target_pairs={{0,1},{1,0},{2,3},{3,2},{4,5},{5,4},{6,7},{7,6},{8,9},{9,8},{10,11... | collective-permute-start | bytes 393224 | tf_op jit(solution)/shard_map/ppermute | solution.py:420
  25.9 4.2 %copy-start = (f32[5120,128]{1,0:T(8,128)S(1)}, f32[5120,128]{1,0:T(8,128)}, u32[]{:S(2)}) copy-start(f32[5120,128]{1,0:T(8,128)} %state_ref.3) | copy-start | bytes 7864324
  25.9 4.2 %copy-start.2 = (f32[2,1024]{1,0:T(2,128)S(1)}, f32[2,1024]{1,0:T(2,128)}, u32[]{:S(2)}) copy-start(f32[2,1024]{1,0:T(2,128)} %gains_ref.1) | copy-start | bytes 24580
  25.9 4.2 %copy-start.3 = (f32[128]{0:T(128)S(1)}, f32[128]{0:T(128)}, u32[]{:S(2)}) copy-start(f32[128]{0:T(128)} %param.14) | copy-start | bytes 1540
  28.6 1.4 %collective-permute-start.2 = (f32[2,24,256]{2,1,0:T(8,128)S(1)}, f32[2,24,256]{2,1,0:T(8,128)S(1)}, u32[]{:S(2)}, u32[]{:S(2)}) collective-permute-start(f32[2,24,256]{2,1,0:T(8,128)S(1)} %get-tuple-element.31), channel_id=1, source_target_pairs={{0,1},{1,0},{2,3},{3,2},{4,5},{5,4},{6,7},{7,6},{8,9},{9,8},{10,11... | collective-permute-start | bytes 147464 | tf_op jit(solution)/shard_map/ppermute | solution.py:420
  62.1 18.0 %copy-start.1 = (s32[2048]{0:T(1024)S(1)}, s32[2048]{0:T(1024)}, u32[]{:S(2)}) copy-start(s32[2048]{0:T(1024)} %param.15) | copy-start | bytes 24580
  62.1 2.0 %collective-permute-start.15 = (bf16[2,2,2,4,64,128]{5,4,3,2,1,0:T(8,128)(2,1)S(1)}, bf16[2,2,2,4,64,128]{5,4,3,2,1,0:T(8,128)(2,1)S(1)}, u32[]{:S(2)}, u32[]{:S(2)}) collective-permute-start(bf16[2,2,2,4,64,128]{5,4,3,2,1,0:T(8,128)(2,1)S(1)} %bitcast.38), channel_id=1, source_target_pairs={{0,1},{1,0},{2,3},{3,2},{4,5},{5,4},{6,7},{7,6},{8,9},{9,8},{10,11... | collective-permute-start | bytes 1572872 | tf_op jit(solution)/shard_map/ppermute | solution.py:420
  62.3 17.7 %collective-permute-start.14 = (bf16[2816,128]{1,0:T(8,128)(2,1)S(1)}, bf16[2816,128]{1,0:T(8,128)(2,1)S(1)}, u32[]{:S(2)}, u32[]{:S(2)}) collective-permute-start(bf16[2816,128]{1,0:T(8,128)(2,1)S(1)} %get-tuple-element.39), channel_id=1, source_target_pairs={{0,1},{1,0},{2,3},{3,2},{4,5},{5,4},{6,7},{7,6},{8,9},{9,8},{10,11... | collective-permute-start | bytes 2162696 | tf_op jit(solution)/shard_map/ppermute | solution.py:420
  64.1 5.6 %collective-permute-start.16 = (bf16[2,4,64,128]{3,2,1,0:T(8,128)(2,1)S(1)}, bf16[2,4,64,128]{3,2,1,0:T(8,128)(2,1)S(1)}, u32[]{:S(2)}, u32[]{:S(2)}) collective-permute-start(bf16[2,4,64,128]{3,2,1,0:T(8,128)(2,1)S(1)} %get-tuple-element.44), channel_id=1, source_target_pairs={{0,2},{1,3},{2,0},{3,1},{4,6},{5,7},{6,4},{7,5},{8,10},{9,11},{10,... | collective-permute-start | bytes 393224 | tf_op jit(solution)/shard_map/ppermute | solution.py:420
  64.2 5.6 %collective-permute-start.17 = (bf16[2,4,64,128]{3,2,1,0:T(8,128)(2,1)S(1)}, bf16[2,4,64,128]{3,2,1,0:T(8,128)(2,1)S(1)}, u32[]{:S(2)}, u32[]{:S(2)}) collective-permute-start(bf16[2,4,64,128]{3,2,1,0:T(8,128)(2,1)S(1)} %get-tuple-element.46), channel_id=1, source_target_pairs={{0,4},{1,5},{2,6},{3,7},{4,0},{5,1},{6,2},{7,3},{8,12},{9,13},{10,... | collective-permute-start | bytes 393224 | tf_op jit(solution)/shard_map/ppermute | solution.py:420
  69.9 4.3 %collective-permute-start.18 = (bf16[4,64,128]{2,1,0:T(8,128)(2,1)S(1)}, bf16[4,64,128]{2,1,0:T(8,128)(2,1)S(1)}, u32[]{:S(2)}, u32[]{:S(2)}) collective-permute-start(bf16[4,64,128]{2,1,0:T(8,128)(2,1)S(1)} %get-tuple-element.48), channel_id=1, source_target_pairs={{0,4},{1,5},{2,6},{3,7},{4,0},{5,1},{6,2},{7,3},{8,12},{9,13},{10,... | collective-permute-start | bytes 196616 | tf_op jit(solution)/shard_map/ppermute | solution.py:420
  71.3 4.3 %collective-permute-start.19 = (bf16[4,64,128]{2,1,0:T(8,128)(2,1)S(1)}, bf16[4,64,128]{2,1,0:T(8,128)(2,1)S(1)}, u32[]{:S(2)}, u32[]{:S(2)}) collective-permute-start(bf16[4,64,128]{2,1,0:T(8,128)(2,1)S(1)} %get-tuple-element.50), channel_id=1, source_target_pairs={{0,2},{1,3},{2,0},{3,1},{4,6},{5,7},{6,4},{7,5},{8,10},{9,11},{10,... | collective-permute-start | bytes 196616 | tf_op jit(solution)/shard_map/ppermute | solution.py:420
  75.6 7.7 %collective-permute-start.20 = (bf16[128,128]{1,0:T(8,128)(2,1)S(1)}, bf16[128,128]{1,0:T(8,128)(2,1)S(1)}, u32[]{:S(2)}, u32[]{:S(2)}) collective-permute-start(bf16[128,128]{1,0:T(8,128)(2,1)S(1)} %get-tuple-element.52), channel_id=1, source_target_pairs={{0,8},{1,9},{2,10},{3,11},{4,12},{5,13},{6,14},{7,15},{8,0},{9,1},... | collective-permute-start | bytes 98312 | tf_op jit(solution)/shard_map/ppermute | solution.py:420
  77.2 6.1 %collective-permute-start.21 = (bf16[128,128]{1,0:T(8,128)(2,1)S(1)}, bf16[128,128]{1,0:T(8,128)(2,1)S(1)}, u32[]{:S(2)}, u32[]{:S(2)}) collective-permute-start(bf16[128,128]{1,0:T(8,128)(2,1)S(1)} %get-tuple-element.53), channel_id=1, source_target_pairs={{0,16},{1,17},{2,18},{3,19},{4,20},{5,21},{6,22},{7,23},{8,24},{9,... | collective-permute-start | bytes 98312 | tf_op jit(solution)/shard_map/ppermute | solution.py:420
  77.2 6.1 %collective-permute-start.22 = (bf16[128,128]{1,0:T(8,128)(2,1)S(1)}, bf16[128,128]{1,0:T(8,128)(2,1)S(1)}, u32[]{:S(2)}, u32[]{:S(2)}) collective-permute-start(bf16[128,128]{1,0:T(8,128)(2,1)S(1)} %get-tuple-element.54), channel_id=1, source_target_pairs={{0,24},{1,25},{2,26},{3,27},{4,28},{5,29},{6,30},{7,31},{8,16},{9,... | collective-permute-start | bytes 98312 | tf_op jit(solution)/shard_map/ppermute | solution.py:420
